TPU v7x, 32 devices: a whole 2x2x4 slice. The times are simulated.
32 devices in a mesh: replica: 2 (over x), model2: 4 (over z), model: 4 (over y, core).
Axes of the slice: x: 2, y: 2, z: 4, core: 2. Of those that a mesh axis runs over, the one named last changes fastest.
Arguments:
- x_prompt: bfloat16 [4, 3, 384, 2048], P('replica'), parts along dimension 0
- lengths: int32 [4, 3], P('replica'), parts along dimension 0
- x_new: bfloat16 [12, 2048], P('replica'), parts along dimension 0
- st_qkv: bfloat16 [4, 2048, 2560], P('model')
- st_out: bfloat16 [4, 2048, 2048], P('model')
- st_gateup: bfloat16 [4, 2048, 11264], P('model')
- st_down_t: bfloat16 [4, 2048, 5632], P('model')
- gain_attn: float32 [4, 2048], replicated
- gain_mlp: float32 [4, 2048], replicated
- tp_query: bfloat16 [4, 2048, 32, 64], P(None, None, ('model', 'model2'))
- tp_key: bfloat16 [4, 2048, 16, 64], P(None, None, ('model', 'model2'))
- tp_value: bfloat16 [4, 2048, 16, 64], P(None, None, ('model', 'model2'))
- tp_out: bfloat16 [4, 32, 64, 2048], P(None, ('model', 'model2'))
- tp_gate: bfloat16 [4, 2048, 5632], P(None, None, ('model', 'model2'))
- tp_up: bfloat16 [4, 2048, 5632], P(None, None, ('model', 'model2'))
- tp_down: bfloat16 [4, 5632, 2048], P(None, ('model', 'model2'))
Outputs:
- output 1: bfloat16 [12, 2048], P('replica'), parts along dimension 0
- output 2: bfloat16 [12, 2048], P('replica'), parts along dimension 0
- output 3: bfloat16 [4, 12, 385, 16, 64], P(None, 'replica', None, ('model', 'model2')), parts along dimension 1
- output 4: bfloat16 [4, 12, 385, 16, 64], P(None, 'replica', None, ('model', 'model2')), parts along dimension 1
There are 2 independent parts. A program takes and returns all parts, laid end to end along the dimension named above; an argument that names none is the same for every part.
All inputs are finite; a program needn't handle non-finite values.
Results may differ from a plain program's by a relative error of at most 0.0165032.
Values are sent between devices in bfloat16 or wider.
A program may use at most 1 GiB of HBM per device.

v0:
```python
import jax
import jax.numpy as jnp
from jax import lax
from jax.sharding import PartitionSpec as P

EPS = 1e-5
THETA = 10000.0
TP_AXES = ('model', 'model2')


def rms_norm(values_in, gain_vec):
    x_f32 = values_in.astype(jnp.float32)
    inv_rms = lax.rsqrt(jnp.mean(x_f32 * x_f32, axis=-1, keepdims=True) + EPS)
    return (x_f32 * inv_rms * gain_vec).astype(jnp.bfloat16)


def rope_angles(positions, head_dim):
    half_dim = head_dim // 2
    inv_freq = jnp.power(THETA, jnp.arange(half_dim, dtype=jnp.float32) * (-2.0 / head_dim))
    angles = positions.astype(jnp.float32)[..., None] * inv_freq
    return jnp.cos(angles), jnp.sin(angles)


def apply_rope(values_in, cos_t, sin_t):
    half_dim = values_in.shape[-1] // 2
    first_half = values_in[..., :half_dim]
    second = values_in[..., half_dim:]
    return jnp.concatenate([first_half * cos_t - second * sin_t, second * cos_t + first_half * sin_t], axis=-1)


def stage_layer(hidden_x, key_mask, cos_t, sin_t, g_attn, g_mlp, w_qkv, w_out, w_gateup, w_down_t, head_dim):
    row_count, seq_len, model_dim = hidden_x.shape
    q_cols = w_out.shape[0]
    num_heads = q_cols // head_dim
    k_cols = (w_qkv.shape[1] - q_cols) // 2
    kv_heads = k_cols // head_dim
    group_size = num_heads // kv_heads
    ff_width = w_down_t.shape[1]
    normed = rms_norm(hidden_x, g_attn)
    proj_all = jnp.einsum('bsd,df->bsf', normed, w_qkv, preferred_element_type=jnp.float32)
    queries = apply_rope(proj_all[..., :q_cols].reshape(row_count, seq_len, kv_heads, group_size, head_dim), cos_t[None, :, None, None, :], sin_t[None, :, None, None, :]).astype(jnp.bfloat16)
    key_rot = apply_rope(proj_all[..., q_cols:q_cols + k_cols].reshape(row_count, seq_len, kv_heads, head_dim), cos_t[None, :, None, :], sin_t[None, :, None, :]).astype(jnp.bfloat16)
    val_proj = proj_all[..., q_cols + k_cols:].reshape(row_count, seq_len, kv_heads, head_dim).astype(jnp.bfloat16)
    scores = jnp.einsum('bqcge,bkce->bcgqk', queries, key_rot, preferred_element_type=jnp.float32) * head_dim ** -0.5
    scores = jnp.where(key_mask[:, None, None], scores, -1e30)
    probs_bf = jax.nn.softmax(scores, axis=-1).astype(jnp.bfloat16)
    attn_out = jnp.einsum('bcgqk,bkce->bqcge', probs_bf, val_proj, preferred_element_type=jnp.float32).astype(jnp.bfloat16).reshape(row_count, seq_len, q_cols)
    resid_mid = (hidden_x.astype(jnp.float32) + jnp.einsum('bsf,fd->bsd', attn_out, w_out, preferred_element_type=jnp.float32)).astype(jnp.bfloat16)
    normed_mlp = rms_norm(resid_mid, g_mlp)
    gate_up = jnp.einsum('bsd,df->bsf', normed_mlp, w_gateup, preferred_element_type=jnp.float32)
    act_out = (jax.nn.silu(gate_up[..., :ff_width]) * gate_up[..., ff_width:]).astype(jnp.bfloat16)
    layer_out = (resid_mid.astype(jnp.float32) + jnp.einsum('bsf,df->bsd', act_out, w_down_t, preferred_element_type=jnp.float32)).astype(jnp.bfloat16)
    return layer_out, key_rot, val_proj


def decode_stack(x_new, len_flat, gain_attn, gain_mlp, tp_query, tp_key, tp_value, tp_out, tp_gate, tp_up, tp_down, k_prompt, v_prompt):
    n_rows = x_new.shape[0]
    head_dim = tp_query.shape[-1]
    per_dev = tp_key.shape[2]
    group_size = tp_query.shape[2] // per_dev
    seq_len = k_prompt.shape[2]
    cos_n, sin_n = rope_angles(len_flat, head_dim)
    cached = jnp.arange(seq_len)[None, :] < len_flat[:, None]
    score_scale = head_dim ** -0.5

    def layer_fn(carry_x, params):
        g_attn, g_mlp, w_query, w_key, w_value, w_outp, w_gate, w_upp, w_down, k_cached, v_cached = params
        normed = rms_norm(carry_x, g_attn)
        queries = apply_rope(jnp.einsum('bd,dhe->bhe', normed, w_query, preferred_element_type=jnp.float32), cos_n[:, None, :], sin_n[:, None, :])
        queries = queries.astype(jnp.bfloat16).reshape(n_rows, per_dev, group_size, head_dim)
        key_new = apply_rope(jnp.einsum('bd,dce->bce', normed, w_key, preferred_element_type=jnp.float32), cos_n[:, None, :], sin_n[:, None, :]).astype(jnp.bfloat16)
        val_new = jnp.einsum('bd,dce->bce', normed, w_value, preferred_element_type=jnp.float32).astype(jnp.bfloat16)
        s_old = jnp.einsum('bcge,bsce->bcgs', queries, k_cached, preferred_element_type=jnp.float32) * score_scale
        s_old = jnp.where(cached[:, None, None, :], s_old, -1e30)
        s_new = jnp.einsum('bcge,bce->bcg', queries, key_new, preferred_element_type=jnp.float32) * score_scale
        row_max = jnp.maximum(jnp.max(s_old, axis=-1), s_new)
        e_old = jnp.exp(s_old - row_max[..., None])
        e_new = jnp.exp(s_new - row_max)
        denom_sum = jnp.sum(e_old, axis=-1) + e_new
        p_old = (e_old / denom_sum[..., None]).astype(jnp.bfloat16)
        p_new = (e_new / denom_sum).astype(jnp.bfloat16)
        attn_out = jnp.einsum('bcgs,bsce->bcge', p_old, v_cached, preferred_element_type=jnp.float32) + p_new.astype(jnp.float32)[..., None] * val_new.astype(jnp.float32)[:, :, None, :]
        attn_out = attn_out.astype(jnp.bfloat16).reshape(n_rows, per_dev * group_size, head_dim)
        part_sum = lax.psum(jnp.einsum('bhe,hed->bd', attn_out, w_outp, preferred_element_type=jnp.float32), TP_AXES)
        resid_mid = (carry_x.astype(jnp.float32) + part_sum).astype(jnp.bfloat16)
        normed_mlp = rms_norm(resid_mid, g_mlp)
        act_out = (jax.nn.silu(jnp.dot(normed_mlp, w_gate, preferred_element_type=jnp.float32)) * jnp.dot(normed_mlp, w_upp, preferred_element_type=jnp.float32)).astype(jnp.bfloat16)
        down_sum = lax.psum(jnp.dot(act_out, w_down, preferred_element_type=jnp.float32), TP_AXES)
        layer_out = (resid_mid.astype(jnp.float32) + down_sum).astype(jnp.bfloat16)
        return layer_out, (key_new, val_new)

    dec_out, new_kv = lax.scan(layer_fn, x_new, (gain_attn, gain_mlp, tp_query, tp_key, tp_value, tp_out, tp_gate, tp_up, tp_down, k_prompt, v_prompt))
    k_full = jnp.concatenate([k_prompt, new_kv[0][:, :, None]], axis=2)
    v_full = jnp.concatenate([v_prompt, new_kv[1][:, :, None]], axis=2)
    return dec_out, k_full, v_full


def solution(mesh):
    stages = mesh.shape['model']
    width = mesh.shape['model2']
    stage_spec = P('model', None, None)
    in_specs = (P('replica', None, None, None), P('replica', None), P('replica', None),
                stage_spec, stage_spec, stage_spec, stage_spec, P(None, None), P(None, None),
                P(None, None, TP_AXES, None), P(None, None, TP_AXES, None), P(None, None, TP_AXES, None),
                P(None, TP_AXES, None, None), P(None, None, TP_AXES), P(None, None, TP_AXES), P(None, TP_AXES, None))
    cache_spec = P(None, 'replica', None, TP_AXES, None)
    out_specs = (P('replica', None), P('replica', None), cache_spec, cache_spec)

    def shard_body(x_prompt, lengths, x_new, st_qkv, st_out, st_gateup, st_down_t, gain_attn, gain_mlp, tp_query, tp_key, tp_value, tp_out, tp_gate, tp_up, tp_down):
        num_micro, row_count, seq_len, model_dim = x_prompt.shape
        batch_rows = num_micro * row_count
        stage_layers = st_qkv.shape[0]
        head_dim = tp_query.shape[-1]
        q_cols = st_out.shape[1]
        kv_heads = (st_qkv.shape[2] - q_cols) // (2 * head_dim)
        per_dev = tp_key.shape[2]
        num_slots = per_dev * stages * width
        stage_idx = lax.axis_index('model')
        col_idx = lax.axis_index('model2')
        stage_g_attn = lax.dynamic_slice_in_dim(gain_attn, stage_idx * stage_layers, stage_layers, 0)
        stage_g_mlp = lax.dynamic_slice_in_dim(gain_mlp, stage_idx * stage_layers, stage_layers, 0)
        positions = jnp.arange(seq_len)
        cos_t, sin_t = rope_angles(positions, head_dim)
        causal = positions[None, :] <= positions[:, None]
        send_pairs = [(i, i + 1) for i in range(stages - 1)]

        def tick_fn(carry, tick_idx):
            recv_act, k_store, v_store, last_rows = carry
            mb_raw = tick_idx - stage_idx
            is_valid = (mb_raw >= 0) & (mb_raw < num_micro)
            mb_idx = jnp.clip(mb_raw, 0, num_micro - 1)
            fresh_act = lax.dynamic_index_in_dim(x_prompt, mb_idx, 0, keepdims=False)
            hidden_x = jnp.where(stage_idx == 0, fresh_act, recv_act)
            len_mb = lax.dynamic_index_in_dim(lengths, mb_idx, 0, keepdims=False)
            key_mask = causal[None] & (positions[None, None, :] < len_mb[:, None, None])
            row_start = mb_idx * row_count
            for layer_idx in range(stage_layers):
                hidden_x, key_rot, val_proj = stage_layer(hidden_x, key_mask, cos_t, sin_t, stage_g_attn[layer_idx], stage_g_mlp[layer_idx], st_qkv[layer_idx], st_out[layer_idx], st_gateup[layer_idx], st_down_t[layer_idx], head_dim)
                corner = (layer_idx, row_start, 0, 0, 0)
                block = (1, row_count, seq_len, kv_heads, head_dim)
                k_store = lax.dynamic_update_slice(k_store, jnp.where(is_valid, key_rot[None], lax.dynamic_slice(k_store, corner, block)), corner)
                v_store = lax.dynamic_update_slice(v_store, jnp.where(is_valid, val_proj[None], lax.dynamic_slice(v_store, corner, block)), corner)
            picked = jnp.take_along_axis(hidden_x, (len_mb - 1)[:, None, None], axis=1)[:, 0]
            old_rows = lax.dynamic_slice_in_dim(last_rows, row_start, row_count, 0)
            keep_last = is_valid & (stage_idx == stages - 1)
            last_rows = lax.dynamic_update_slice_in_dim(last_rows, jnp.where(keep_last, picked, old_rows), row_start, 0)
            recv_act = lax.ppermute(hidden_x, 'model', send_pairs)
            return (recv_act, k_store, v_store, last_rows), None

        kv_shape = (stage_layers, batch_rows, seq_len, kv_heads, head_dim)
        init_carry = (jnp.zeros((row_count, seq_len, model_dim), jnp.bfloat16), jnp.zeros(kv_shape, jnp.bfloat16), jnp.zeros(kv_shape, jnp.bfloat16), jnp.zeros((batch_rows, model_dim), jnp.bfloat16))
        final_carry = lax.scan(tick_fn, init_carry, jnp.arange(num_micro + stages - 1))[0]
        last_hidden = lax.psum(final_carry[3], 'model')

        def regroup(store):
            wide_view = jnp.broadcast_to(store[:, :, :, :, None, :], (stage_layers, batch_rows, seq_len, kv_heads, num_slots // kv_heads, head_dim))
            wide_view = wide_view.reshape(stage_layers, batch_rows, seq_len, stages, width, per_dev, head_dim)
            mine_sel = lax.dynamic_index_in_dim(wide_view, col_idx, axis=4, keepdims=False)
            moved_kv = lax.all_to_all(mine_sel, 'model', 3, 0, tiled=True)
            return moved_kv.reshape(stages * stage_layers, batch_rows, seq_len, per_dev, head_dim)

        k_mine = regroup(final_carry[1])
        v_mine = regroup(final_carry[2])
        dec_out, k_full, v_full = decode_stack(x_new, lengths.reshape(batch_rows), gain_attn, gain_mlp, tp_query, tp_key, tp_value, tp_out, tp_gate, tp_up, tp_down, k_mine, v_mine)
        return dec_out, last_hidden, k_full, v_full

    return jax.shard_map(shard_body, mesh=mesh, in_specs=in_specs, out_specs=out_specs, check_vma=False)
```

profile of v0, /device:TPU:0, one launch (start us, length us, event | category | flops | bytes accessed | tf_op | source)
XLA Modules:
  0.0 1977.1 jit_solution(632677598855856050)
XLA Ops:
  9.4 1350.0 %while.40 = (s32[]{:T(128)}, bf16[3,384,2048]{2,1,0:T(8,128)(2,1)}, bf16[1,6,384,4,64]{2,4,1,3,0:T(8,128)(2,1)}, bf16[1,6,384,4,64]{2,4,1,3,0:T(8,128)(2,1)}, bf...) while((s32[]{:T(128)}, bf16[3,384,2048]{2,1,0:T(8,128)(2,1)}, ...), condition=%wide.region_5.6_spmd.clone.clone.clone, body=%wide.region_0.5_spmd.clone.clone.clone.sunk | while | flops 107156930560 | bytes 479197568 | solution.py:152
  35.6 4.6 fusion.249
  40.3 17.1 fusion.250
  57.4 4.8 slice.207
  66.2 9.8 copy.138
  77.3 6.0 subtract_convert_fusion.7
  84.5 20.3 %fusion.251 = f32[3,4,8,384]{3,2,1,0:T(8,128)} fusion(pred[3,384,384]{1,2,0:T(8,128)(4,1)} %broadcast_and_fusion.2, bf16[3,384,4,8,32]{1,4,3,2,0:T(8,128)(2,1)} %get-tuple-element.1205, bf16[3,384,4,8,32]{1,4,3,2,0:T(8,128)(2,1)} %get-tuple-element.1206, bf16[3,384,4,32]{1,3,2,0:T(8,128)(2,1)S(1)} %get-tuple-element.1207, ...), kind=kOutput, calls=%fused_computation.193.clone.1 | convolution fusion | flops 1879179648 | bytes 5898240 | tf_op jit(solution)/shard_map/while/body/eval_jaxpr/sub | solution.py:46
  104.9 25.6 %fusion.252 = bf16[3,4,64,8,384]{4,2,3,1,0:T(8,128)(2,1)} fusion(bf16[3,384,4,64,1]{1,3,4,2,0:T(8,128)(2,1)S(1)} %bitcast.303, f32[3,4,8,384]{3,2,1,0:T(8,128)} %fusion.251, pred[3,384,384]{1,2,0:T(8,128)(4,1)} %broadcast_and_fusion.2, bf16[3,384,4,8,32]{1,4,3,2,0:T(8,128)(2,1)} %get-tuple-element.1205, ...), kind=kOutput, calls=%fused_computation.149.clone.1 | convolution fusion | flops 3707671040 | bytes 11206656 | tf_op jit(solution)/shard_map/while/body/eval_jaxpr/bcgqk,bkce->bqcge/dot_general | solution.py:47
  130.5 15.3 fusion.253
  145.9 62.4 %fusion.254 = f32[3,384,11264]{2,1,0:T(8,128)} fusion(bf16[1,2048,11264]{2,1,0:T(8,128)(2,1)} %get-tuple-element.1276, bf16[3,384,2048]{2,1,0:T(8,128)(2,1)S(1)} %get-tuple-element.1209, f32[2048]{0:T(1024)S(1)} %bitcast.324, f32[3,384]{1,0:T(4,128)S(1)} %add_rsqrt_fusion.11), kind=kOutput, calls=%fused_computation.111.clone.2 | convolution fusion | flops 53159657472 | bytes 102773248 | tf_op jit(solution)/shard_map/while/body/eval_jaxpr/bsd,df->bsf/dot_general | solution.py:50
  208.3 41.1 %fusion.255 = bf16[3,384,2048]{2,1,0:T(8,128)(2,1)} fusion(bf16[3,384,2048]{2,1,0:T(8,128)(2,1)} %copy-done.19, bf16[1,2048,5632]{2,1,0:T(8,128)(2,1)} %get-tuple-element.1277, f32[3,384,11264]{2,1,0:T(8,128)} %fusion.254), kind=kOutput, calls=%fused_computation.137.clone.2 | convolution fusion | flops 26621116416 | bytes 84410368 | tf_op jit(solution)/shard_map/while/body/eval_jaxpr/bsf,df->bsd/dot_general | solution.py:52
  249.4 6.0 collective-permute-start
  270.4 17.1 fusion.250
  287.6 4.8 slice.207
  296.3 9.8 copy.138
  307.4 6.0 subtract_convert_fusion.7
  314.7 20.3 %fusion.251 = f32[3,4,8,384]{3,2,1,0:T(8,128)} fusion(pred[3,384,384]{1,2,0:T(8,128)(4,1)} %broadcast_and_fusion.2, bf16[3,384,4,8,32]{1,4,3,2,0:T(8,128)(2,1)} %get-tuple-element.1205, bf16[3,384,4,8,32]{1,4,3,2,0:T(8,128)(2,1)} %get-tuple-element.1206, bf16[3,384,4,32]{1,3,2,0:T(8,128)(2,1)S(1)} %get-tuple-element.1207, ...), kind=kOutput, calls=%fused_computation.193.clone.1 | convolution fusion | flops 1879179648 | bytes 5898240 | tf_op jit(solution)/shard_map/while/body/eval_jaxpr/sub | solution.py:46
  335.0 25.6 %fusion.252 = bf16[3,4,64,8,384]{4,2,3,1,0:T(8,128)(2,1)} fusion(bf16[3,384,4,64,1]{1,3,4,2,0:T(8,128)(2,1)S(1)} %bitcast.303, f32[3,4,8,384]{3,2,1,0:T(8,128)} %fusion.251, pred[3,384,384]{1,2,0:T(8,128)(4,1)} %broadcast_and_fusion.2, bf16[3,384,4,8,32]{1,4,3,2,0:T(8,128)(2,1)} %get-tuple-element.1205, ...), kind=kOutput, calls=%fused_computation.149.clone.1 | convolution fusion | flops 3707671040 | bytes 11206656 | tf_op jit(solution)/shard_map/while/body/eval_jaxpr/bcgqk,bkce->bqcge/dot_general | solution.py:47
  360.6 15.3 fusion.253
  376.0 62.4 %fusion.254 = f32[3,384,11264]{2,1,0:T(8,128)} fusion(bf16[1,2048,11264]{2,1,0:T(8,128)(2,1)} %get-tuple-element.1276, bf16[3,384,2048]{2,1,0:T(8,128)(2,1)S(1)} %get-tuple-element.1209, f32[2048]{0:T(1024)S(1)} %bitcast.324, f32[3,384]{1,0:T(4,128)S(1)} %add_rsqrt_fusion.11), kind=kOutput, calls=%fused_computation.111.clone.2 | convolution fusion | flops 53159657472 | bytes 102773248 | tf_op jit(solution)/shard_map/while/body/eval_jaxpr/bsd,df->bsf/dot_general | solution.py:50
  438.5 41.1 %fusion.255 = bf16[3,384,2048]{2,1,0:T(8,128)(2,1)} fusion(bf16[3,384,2048]{2,1,0:T(8,128)(2,1)} %copy-done.19, bf16[1,2048,5632]{2,1,0:T(8,128)(2,1)} %get-tuple-element.1277, f32[3,384,11264]{2,1,0:T(8,128)} %fusion.254), kind=kOutput, calls=%fused_computation.137.clone.2 | convolution fusion | flops 26621116416 | bytes 84410368 | tf_op jit(solution)/shard_map/while/body/eval_jaxpr/bsf,df->bsd/dot_general | solution.py:52
  479.6 49.2 %collective-permute-start = (bf16[3,384,2048]{2,1,0:T(8,128)(2,1)}, bf16[3,384,2048]{2,1,0:T(8,128)(2,1)}, u32[]{:S(2)}, u32[]{:S(2)}) collective-permute-start(bf16[3,384,2048]{2,1,0:T(8,128)(2,1)} %fusion.255), channel_id=1, source_target_pairs={{0,1},{1,2},{2,3},{4,5},{5,6},{6,7},{8,9},{9,10},{10,11},{12,13},{... | collective-permute-start | bytes 14155784 | tf_op jit(solution)/shard_map/while/body/eval_jaxpr/ppermute | solution.py:147
  539.1 4.6 fusion.249
  543.7 17.0 fusion.250
  560.9 4.8 slice.207
  569.7 9.8 copy.138
  580.8 6.0 subtract_convert_fusion.7
  588.0 20.3 %fusion.251 = f32[3,4,8,384]{3,2,1,0:T(8,128)} fusion(pred[3,384,384]{1,2,0:T(8,128)(4,1)} %broadcast_and_fusion.2, bf16[3,384,4,8,32]{1,4,3,2,0:T(8,128)(2,1)} %get-tuple-element.1205, bf16[3,384,4,8,32]{1,4,3,2,0:T(8,128)(2,1)} %get-tuple-element.1206, bf16[3,384,4,32]{1,3,2,0:T(8,128)(2,1)S(1)} %get-tuple-element.1207, ...), kind=kOutput, calls=%fused_computation.193.clone.1 | convolution fusion | flops 1879179648 | bytes 5898240 | tf_op jit(solution)/shard_map/while/body/eval_jaxpr/sub | solution.py:46
  608.4 25.6 %fusion.252 = bf16[3,4,64,8,384]{4,2,3,1,0:T(8,128)(2,1)} fusion(bf16[3,384,4,64,1]{1,3,4,2,0:T(8,128)(2,1)S(1)} %bitcast.303, f32[3,4,8,384]{3,2,1,0:T(8,128)} %fusion.251, pred[3,384,384]{1,2,0:T(8,128)(4,1)} %broadcast_and_fusion.2, bf16[3,384,4,8,32]{1,4,3,2,0:T(8,128)(2,1)} %get-tuple-element.1205, ...), kind=kOutput, calls=%fused_computation.149.clone.1 | convolution fusion | flops 3707671040 | bytes 11206656 | tf_op jit(solution)/shard_map/while/body/eval_jaxpr/bcgqk,bkce->bqcge/dot_general | solution.py:47
  633.9 15.3 fusion.253
  649.3 62.4 %fusion.254 = f32[3,384,11264]{2,1,0:T(8,128)} fusion(bf16[1,2048,11264]{2,1,0:T(8,128)(2,1)} %get-tuple-element.1276, bf16[3,384,2048]{2,1,0:T(8,128)(2,1)S(1)} %get-tuple-element.1209, f32[2048]{0:T(1024)S(1)} %bitcast.324, f32[3,384]{1,0:T(4,128)S(1)} %add_rsqrt_fusion.11), kind=kOutput, calls=%fused_computation.111.clone.2 | convolution fusion | flops 53159657472 | bytes 102773248 | tf_op jit(solution)/shard_map/while/body/eval_jaxpr/bsd,df->bsf/dot_general | solution.py:50
  711.8 41.1 %fusion.255 = bf16[3,384,2048]{2,1,0:T(8,128)(2,1)} fusion(bf16[3,384,2048]{2,1,0:T(8,128)(2,1)} %copy-done.19, bf16[1,2048,5632]{2,1,0:T(8,128)(2,1)} %get-tuple-element.1277, f32[3,384,11264]{2,1,0:T(8,128)} %fusion.254), kind=kOutput, calls=%fused_computation.137.clone.2 | convolution fusion | flops 26621116416 | bytes 84410368 | tf_op jit(solution)/shard_map/while/body/eval_jaxpr/bsf,df->bsd/dot_general | solution.py:52
  752.9 49.1 %collective-permute-start = (bf16[3,384,2048]{2,1,0:T(8,128)(2,1)}, bf16[3,384,2048]{2,1,0:T(8,128)(2,1)}, u32[]{:S(2)}, u32[]{:S(2)}) collective-permute-start(bf16[3,384,2048]{2,1,0:T(8,128)(2,1)} %fusion.255), channel_id=1, source_target_pairs={{0,1},{1,2},{2,3},{4,5},{5,6},{6,7},{8,9},{9,10},{10,11},{12,13},{... | collective-permute-start | bytes 14155784 | tf_op jit(solution)/shard_map/while/body/eval_jaxpr/ppermute | solution.py:147
  817.0 17.0 fusion.250
  834.1 4.8 slice.207
  842.9 9.8 copy.138
  854.0 6.0 subtract_convert_fusion.7
  861.2 20.3 %fusion.251 = f32[3,4,8,384]{3,2,1,0:T(8,128)} fusion(pred[3,384,384]{1,2,0:T(8,128)(4,1)} %broadcast_and_fusion.2, bf16[3,384,4,8,32]{1,4,3,2,0:T(8,128)(2,1)} %get-tuple-element.1205, bf16[3,384,4,8,32]{1,4,3,2,0:T(8,128)(2,1)} %get-tuple-element.1206, bf16[3,384,4,32]{1,3,2,0:T(8,128)(2,1)S(1)} %get-tuple-element.1207, ...), kind=kOutput, calls=%fused_computation.193.clone.1 | convolution fusion | flops 1879179648 | bytes 5898240 | tf_op jit(solution)/shard_map/while/body/eval_jaxpr/sub | solution.py:46
  881.6 25.6 %fusion.252 = bf16[3,4,64,8,384]{4,2,3,1,0:T(8,128)(2,1)} fusion(bf16[3,384,4,64,1]{1,3,4,2,0:T(8,128)(2,1)S(1)} %bitcast.303, f32[3,4,8,384]{3,2,1,0:T(8,128)} %fusion.251, pred[3,384,384]{1,2,0:T(8,128)(4,1)} %broadcast_and_fusion.2, bf16[3,384,4,8,32]{1,4,3,2,0:T(8,128)(2,1)} %get-tuple-element.1205, ...), kind=kOutput, calls=%fused_computation.149.clone.1 | convolution fusion | flops 3707671040 | bytes 11206656 | tf_op jit(solution)/shard_map/while/body/eval_jaxpr/bcgqk,bkce->bqcge/dot_general | solution.py:47
  907.2 15.3 fusion.253
  922.6 62.4 %fusion.254 = f32[3,384,11264]{2,1,0:T(8,128)} fusion(bf16[1,2048,11264]{2,1,0:T(8,128)(2,1)} %get-tuple-element.1276, bf16[3,384,2048]{2,1,0:T(8,128)(2,1)S(1)} %get-tuple-element.1209, f32[2048]{0:T(1024)S(1)} %bitcast.324, f32[3,384]{1,0:T(4,128)S(1)} %add_rsqrt_fusion.11), kind=kOutput, calls=%fused_computation.111.clone.2 | convolution fusion | flops 53159657472 | bytes 102773248 | tf_op jit(solution)/shard_map/while/body/eval_jaxpr/bsd,df->bsf/dot_general | solution.py:50
  985.0 41.1 %fusion.255 = bf16[3,384,2048]{2,1,0:T(8,128)(2,1)} fusion(bf16[3,384,2048]{2,1,0:T(8,128)(2,1)} %copy-done.19, bf16[1,2048,5632]{2,1,0:T(8,128)(2,1)} %get-tuple-element.1277, f32[3,384,11264]{2,1,0:T(8,128)} %fusion.254), kind=kOutput, calls=%fused_computation.137.clone.2 | convolution fusion | flops 26621116416 | bytes 84410368 | tf_op jit(solution)/shard_map/while/body/eval_jaxpr/bsf,df->bsd/dot_general | solution.py:52
  1026.1 49.1 %collective-permute-start = (bf16[3,384,2048]{2,1,0:T(8,128)(2,1)}, bf16[3,384,2048]{2,1,0:T(8,128)(2,1)}, u32[]{:S(2)}, u32[]{:S(2)}) collective-permute-start(bf16[3,384,2048]{2,1,0:T(8,128)(2,1)} %fusion.255), channel_id=1, source_target_pairs={{0,1},{1,2},{2,3},{4,5},{5,6},{6,7},{8,9},{9,10},{10,11},{12,13},{... | collective-permute-start | bytes 14155784 | tf_op jit(solution)/shard_map/while/body/eval_jaxpr/ppermute | solution.py:147
  1090.2 17.0 fusion.250
  1107.4 4.8 slice.207
  1116.2 9.8 copy.138
  1127.3 6.0 subtract_convert_fusion.7
  1134.5 20.3 %fusion.251 = f32[3,4,8,384]{3,2,1,0:T(8,128)} fusion(pred[3,384,384]{1,2,0:T(8,128)(4,1)} %broadcast_and_fusion.2, bf16[3,384,4,8,32]{1,4,3,2,0:T(8,128)(2,1)} %get-tuple-element.1205, bf16[3,384,4,8,32]{1,4,3,2,0:T(8,128)(2,1)} %get-tuple-element.1206, bf16[3,384,4,32]{1,3,2,0:T(8,128)(2,1)S(1)} %get-tuple-element.1207, ...), kind=kOutput, calls=%fused_computation.193.clone.1 | convolution fusion | flops 1879179648 | bytes 5898240 | tf_op jit(solution)/shard_map/while/body/eval_jaxpr/sub | solution.py:46
  1154.9 25.6 %fusion.252 = bf16[3,4,64,8,384]{4,2,3,1,0:T(8,128)(2,1)} fusion(bf16[3,384,4,64,1]{1,3,4,2,0:T(8,128)(2,1)S(1)} %bitcast.303, f32[3,4,8,384]{3,2,1,0:T(8,128)} %fusion.251, pred[3,384,384]{1,2,0:T(8,128)(4,1)} %broadcast_and_fusion.2, bf16[3,384,4,8,32]{1,4,3,2,0:T(8,128)(2,1)} %get-tuple-element.1205, ...), kind=kOutput, calls=%fused_computation.149.clone.1 | convolution fusion | flops 3707671040 | bytes 11206656 | tf_op jit(solution)/shard_map/while/body/eval_jaxpr/bcgqk,bkce->bqcge/dot_general | solution.py:47
  1180.4 15.3 fusion.253
  1195.8 62.4 %fusion.254 = f32[3,384,11264]{2,1,0:T(8,128)} fusion(bf16[1,2048,11264]{2,1,0:T(8,128)(2,1)} %get-tuple-element.1276, bf16[3,384,2048]{2,1,0:T(8,128)(2,1)S(1)} %get-tuple-element.1209, f32[2048]{0:T(1024)S(1)} %bitcast.324, f32[3,384]{1,0:T(4,128)S(1)} %add_rsqrt_fusion.11), kind=kOutput, calls=%fused_computation.111.clone.2 | convolution fusion | flops 53159657472 | bytes 102773248 | tf_op jit(solution)/shard_map/while/body/eval_jaxpr/bsd,df->bsf/dot_general | solution.py:50
  1258.3 41.1 %fusion.255 = bf16[3,384,2048]{2,1,0:T(8,128)(2,1)} fusion(bf16[3,384,2048]{2,1,0:T(8,128)(2,1)} %copy-done.19, bf16[1,2048,5632]{2,1,0:T(8,128)(2,1)} %get-tuple-element.1277, f32[3,384,11264]{2,1,0:T(8,128)} %fusion.254), kind=kOutput, calls=%fused_computation.137.clone.2 | convolution fusion | flops 26621116416 | bytes 84410368 | tf_op jit(solution)/shard_map/while/body/eval_jaxpr/bsf,df->bsd/dot_general | solution.py:52
  1299.4 49.1 %collective-permute-start = (bf16[3,384,2048]{2,1,0:T(8,128)(2,1)}, bf16[3,384,2048]{2,1,0:T(8,128)(2,1)}, u32[]{:S(2)}, u32[]{:S(2)}) collective-permute-start(bf16[3,384,2048]{2,1,0:T(8,128)(2,1)} %fusion.255), channel_id=1, source_target_pairs={{0,1},{1,2},{2,3},{4,5},{5,6},{6,7},{8,9},{9,10},{10,11},{12,13},{... | collective-permute-start | bytes 14155784 | tf_op jit(solution)/shard_map/while/body/eval_jaxpr/ppermute | solution.py:147
  1359.5 63.2 %all_to_all.30 = bf16[1,6,384,4,1,64]{2,5,1,4,0,3:T(8,128)(2,1)S(1)} all-to-all(bf16[1,6,384,4,1,64]{2,5,1,4,0,3:T(8,128)(2,1)} %bitcast.307), channel_id=1, replica_groups=mesh['replica'=2,'model2'=4,'model'=4] {'model'}, dimensions={3} | all-to-all | bytes 2359296 | tf_op jit(solution)/shard_map/all_to_all | solution.py:159
  1427.0 21.3 %psum.21 = bf16[6,2048]{1,0:T(8,128)(2,1)} all-reduce(bf16[6,2048]{1,0:T(8,128)(2,1)S(1)} %copy-done.16), channel_id=1, replica_groups=mesh['replica'=2,'model2'=4,'model'=4] {'model'}, use_global_device_ids=true, to_apply=%region_14.15 | all-reduce | flops 12288 | bytes 49152 | tf_op jit(solution)/shard_map/psum | solution.py:153
  1448.3 525.2 %while.39 = (s32[]{:T(128)}, bf16[6,2048]{1,0:T(8,128)(2,1)S(1)}, bf16[4,6,1,64]{3,1,2,0:T(8,128)(2,1)S(1)}, bf16[4,6,1,64]{3,1,2,0:T(8,128)(2,1)S(1)}, f32[4,20...) while((s32[]{:T(128)}, bf16[6,2048]{1,0:T(8,128)(2,1)S(1)}, ...), condition=%wide.region_13.14_spmd.clone.clone, body=%wide.region_6.13_spmd.clone.clone.sunk | while | flops 37054560 | bytes 7338349 | solution.py:92
  1457.8 61.0 %psum.28 = f32[6,2048]{1,0:T(8,128)S(1)} all-reduce(f32[6,2048]{1,0:T(8,128)S(1)} %convolution_bitcast_fusion.5), channel_id=1, replica_groups=mesh['replica'=2,'model2'=4,'model'=4] {'model','model2'}, use_global_device_ids=true, to_apply=%region_10.10 | all-reduce | flops 12288 | bytes 98304 | tf_op jit(solution)/shard_map/while/body/eval_jaxpr/psum | solution.py:84
  1523.7 58.0 %psum.29 = f32[6,2048]{1,0:T(8,128)S(1)} all-reduce(f32[6,2048]{1,0:T(8,128)S(1)} %fusion.239), channel_id=1, replica_groups=mesh['replica'=2,'model2'=4,'model'=4] {'model','model2'}, use_global_device_ids=true, to_apply=%region_12.12 | all-reduce | flops 12288 | bytes 98304 | tf_op jit(solution)/shard_map/while/body/eval_jaxpr/psum | solution.py:88
  1591.2 58.2 %psum.28 = f32[6,2048]{1,0:T(8,128)S(1)} all-reduce(f32[6,2048]{1,0:T(8,128)S(1)} %convolution_bitcast_fusion.5), channel_id=1, replica_groups=mesh['replica'=2,'model2'=4,'model'=4] {'model','model2'}, use_global_device_ids=true, to_apply=%region_10.10 | all-reduce | flops 12288 | bytes 98304 | tf_op jit(solution)/shard_map/while/body/eval_jaxpr/psum | solution.py:84
  1654.3 58.0 %psum.29 = f32[6,2048]{1,0:T(8,128)S(1)} all-reduce(f32[6,2048]{1,0:T(8,128)S(1)} %fusion.239), channel_id=1, replica_groups=mesh['replica'=2,'model2'=4,'model'=4] {'model','model2'}, use_global_device_ids=true, to_apply=%region_12.12 | all-reduce | flops 12288 | bytes 98304 | tf_op jit(solution)/shard_map/while/body/eval_jaxpr/psum | solution.py:88
  1721.8 58.2 %psum.28 = f32[6,2048]{1,0:T(8,128)S(1)} all-reduce(f32[6,2048]{1,0:T(8,128)S(1)} %convolution_bitcast_fusion.5), channel_id=1, replica_groups=mesh['replica'=2,'model2'=4,'model'=4] {'model','model2'}, use_global_device_ids=true, to_apply=%region_10.10 | all-reduce | flops 12288 | bytes 98304 | tf_op jit(solution)/shard_map/while/body/eval_jaxpr/psum | solution.py:84
  1784.9 58.0 %psum.29 = f32[6,2048]{1,0:T(8,128)S(1)} all-reduce(f32[6,2048]{1,0:T(8,128)S(1)} %fusion.239), channel_id=1, replica_groups=mesh['replica'=2,'model2'=4,'model'=4] {'model','model2'}, use_global_device_ids=true, to_apply=%region_12.12 | all-reduce | flops 12288 | bytes 98304 | tf_op jit(solution)/shard_map/while/body/eval_jaxpr/psum | solution.py:88
  1852.4 58.2 %psum.28 = f32[6,2048]{1,0:T(8,128)S(1)} all-reduce(f32[6,2048]{1,0:T(8,128)S(1)} %convolution_bitcast_fusion.5), channel_id=1, replica_groups=mesh['replica'=2,'model2'=4,'model'=4] {'model','model2'}, use_global_device_ids=true, to_apply=%region_10.10 | all-reduce | flops 12288 | bytes 98304 | tf_op jit(solution)/shard_map/while/body/eval_jaxpr/psum | solution.py:84
  1915.5 58.0 %psum.29 = f32[6,2048]{1,0:T(8,128)S(1)} all-reduce(f32[6,2048]{1,0:T(8,128)S(1)} %fusion.239), channel_id=1, replica_groups=mesh['replica'=2,'model2'=4,'model'=4] {'model','model2'}, use_global_device_ids=true, to_apply=%region_12.12 | all-reduce | flops 12288 | bytes 98304 | tf_op jit(solution)/shard_map/while/body/eval_jaxpr/psum | solution.py:88
  (426 shorter events, 168.5 us)
Async XLA Ops:
  33.1 112.8 %copy-start.17 = (f32[1,2048]{1,0:T(1,128)}, f32[1,2048]{1,0:T(1,128)S(1)}, u32[]{:S(2)}) copy-start(f32[1,2048]{1,0:T(1,128)S(1)} %get-tuple-element.1275) | copy-start | bytes 24580 | tf_op jit(solution)/shard_map/while
  40.2 17.1 copy-start.1
  66.2 38.7 %copy-start.3 = (bf16[3,384,256]{1,2,0:T(8,128)(2,1)}, bf16[3,384,256]{1,2,0:T(8,128)(2,1)S(1)}, u32[]{:S(2)}) copy-start(bf16[3,384,256]{1,2,0:T(8,128)(2,1)S(1)} %copy.137) | copy-start | bytes 1769476 | tf_op jit(solution)/shard_map/while
  83.5 21.4 %copy-start.5 = (bf16[3,384,4,32]{1,3,2,0:T(8,128)(2,1)}, bf16[3,384,4,32]{1,3,2,0:T(8,128)(2,1)S(1)}, u32[]{:S(2)}) copy-start(bf16[3,384,4,32]{1,3,2,0:T(8,128)(2,1)S(1)} %get-tuple-element.1208) | copy-start | bytes 884740 | tf_op jit(solution)/shard_map/while
  83.5 21.4 %copy-start.7 = (bf16[3,384,4,32]{1,3,2,0:T(8,128)(2,1)}, bf16[3,384,4,32]{1,3,2,0:T(8,128)(2,1)S(1)}, u32[]{:S(2)}) copy-start(bf16[3,384,4,32]{1,3,2,0:T(8,128)(2,1)S(1)} %get-tuple-element.1207) | copy-start | bytes 884740 | tf_op jit(solution)/shard_map/while
  84.5 20.4 %copy-start.2 = (bf16[3,384,4,8,32]{1,4,3,2,0:T(8,128)(2,1)S(1)}, bf16[3,384,4,8,32]{1,4,3,2,0:T(8,128)(2,1)}, u32[]{:S(2)}) copy-start(bf16[3,384,4,8,32]{1,4,3,2,0:T(8,128)(2,1)} %get-tuple-element.1206) | copy-start | bytes 7077892 | tf_op jit(solution)/shard_map/while
  145.8 62.5 %copy-start.19 = (bf16[3,384,2048]{2,1,0:T(8,128)(2,1)}, bf16[3,384,2048]{2,1,0:T(8,128)(2,1)S(1)}, u32[]{:S(2)}) copy-start(bf16[3,384,2048]{2,1,0:T(8,128)(2,1)S(1)} %get-tuple-element.1209) | copy-start | bytes 14155780 | tf_op jit(solution)/shard_map/while
  208.3 52.8 %copy-start.9 = (bf16[1,6,384,4,64]{2,4,1,3,0:T(8,128)(2,1)S(1)}, bf16[1,6,384,4,64]{2,4,1,3,0:T(8,128)(2,1)}, u32[]{:S(2)}) copy-start(bf16[1,6,384,4,64]{2,4,1,3,0:T(8,128)(2,1)} %get-tuple-element.1241) | copy-start | bytes 3538948 | tf_op jit(solution)/shard_map/while
  208.3 52.9 %copy-start.11 = (bf16[1,6,384,4,64]{2,4,1,3,0:T(8,128)(2,1)S(1)}, bf16[1,6,384,4,64]{2,4,1,3,0:T(8,128)(2,1)}, u32[]{:S(2)}) copy-start(bf16[1,6,384,4,64]{2,4,1,3,0:T(8,128)(2,1)} %get-tuple-element.1240) | copy-start | bytes 3538948 | tf_op jit(solution)/shard_map/while
  208.3 53.0 %copy-start.4 = (bf16[3,384,256]{1,2,0:T(8,128)(2,1)S(1)}, bf16[3,384,256]{1,2,0:T(8,128)(2,1)}, u32[]{:S(2)}) copy-start(bf16[3,384,256]{1,2,0:T(8,128)(2,1)} %copy-done.3) | copy-start | bytes 1769476 | tf_op jit(solution)/shard_map/while
  208.3 53.0 %copy-start.6 = (bf16[3,384,4,32]{1,3,2,0:T(8,128)(2,1)S(1)}, bf16[3,384,4,32]{1,3,2,0:T(8,128)(2,1)}, u32[]{:S(2)}) copy-start(bf16[3,384,4,32]{1,3,2,0:T(8,128)(2,1)} %copy-done.5) | copy-start | bytes 884740 | tf_op jit(solution)/shard_map/while
  208.3 53.0 %copy-start.8 = (bf16[3,384,4,32]{1,3,2,0:T(8,128)(2,1)S(1)}, bf16[3,384,4,32]{1,3,2,0:T(8,128)(2,1)}, u32[]{:S(2)}) copy-start(bf16[3,384,4,32]{1,3,2,0:T(8,128)(2,1)} %copy-done.7) | copy-start | bytes 884740 | tf_op jit(solution)/shard_map/while
  249.4 12.4 collective-permute-start
  263.2 112.8 %copy-start.17 = (f32[1,2048]{1,0:T(1,128)}, f32[1,2048]{1,0:T(1,128)S(1)}, u32[]{:S(2)}) copy-start(f32[1,2048]{1,0:T(1,128)S(1)} %get-tuple-element.1275) | copy-start | bytes 24580 | tf_op jit(solution)/shard_map/while
  296.3 38.7 %copy-start.3 = (bf16[3,384,256]{1,2,0:T(8,128)(2,1)}, bf16[3,384,256]{1,2,0:T(8,128)(2,1)S(1)}, u32[]{:S(2)}) copy-start(bf16[3,384,256]{1,2,0:T(8,128)(2,1)S(1)} %copy.137) | copy-start | bytes 1769476 | tf_op jit(solution)/shard_map/while
  313.6 21.4 %copy-start.5 = (bf16[3,384,4,32]{1,3,2,0:T(8,128)(2,1)}, bf16[3,384,4,32]{1,3,2,0:T(8,128)(2,1)S(1)}, u32[]{:S(2)}) copy-start(bf16[3,384,4,32]{1,3,2,0:T(8,128)(2,1)S(1)} %get-tuple-element.1208) | copy-start | bytes 884740 | tf_op jit(solution)/shard_map/while
  313.6 21.4 %copy-start.7 = (bf16[3,384,4,32]{1,3,2,0:T(8,128)(2,1)}, bf16[3,384,4,32]{1,3,2,0:T(8,128)(2,1)S(1)}, u32[]{:S(2)}) copy-start(bf16[3,384,4,32]{1,3,2,0:T(8,128)(2,1)S(1)} %get-tuple-element.1207) | copy-start | bytes 884740 | tf_op jit(solution)/shard_map/while
  314.7 20.4 %copy-start.2 = (bf16[3,384,4,8,32]{1,4,3,2,0:T(8,128)(2,1)S(1)}, bf16[3,384,4,8,32]{1,4,3,2,0:T(8,128)(2,1)}, u32[]{:S(2)}) copy-start(bf16[3,384,4,8,32]{1,4,3,2,0:T(8,128)(2,1)} %get-tuple-element.1206) | copy-start | bytes 7077892 | tf_op jit(solution)/shard_map/while
  376.0 62.5 %copy-start.19 = (bf16[3,384,2048]{2,1,0:T(8,128)(2,1)}, bf16[3,384,2048]{2,1,0:T(8,128)(2,1)S(1)}, u32[]{:S(2)}) copy-start(bf16[3,384,2048]{2,1,0:T(8,128)(2,1)S(1)} %get-tuple-element.1209) | copy-start | bytes 14155780 | tf_op jit(solution)/shard_map/while
  438.4 96.0 %copy-start.9 = (bf16[1,6,384,4,64]{2,4,1,3,0:T(8,128)(2,1)S(1)}, bf16[1,6,384,4,64]{2,4,1,3,0:T(8,128)(2,1)}, u32[]{:S(2)}) copy-start(bf16[1,6,384,4,64]{2,4,1,3,0:T(8,128)(2,1)} %get-tuple-element.1241) | copy-start | bytes 3538948 | tf_op jit(solution)/shard_map/while
  438.4 96.1 %copy-start.11 = (bf16[1,6,384,4,64]{2,4,1,3,0:T(8,128)(2,1)S(1)}, bf16[1,6,384,4,64]{2,4,1,3,0:T(8,128)(2,1)}, u32[]{:S(2)}) copy-start(bf16[1,6,384,4,64]{2,4,1,3,0:T(8,128)(2,1)} %get-tuple-element.1240) | copy-start | bytes 3538948 | tf_op jit(solution)/shard_map/while
  438.4 96.2 %copy-start.4 = (bf16[3,384,256]{1,2,0:T(8,128)(2,1)S(1)}, bf16[3,384,256]{1,2,0:T(8,128)(2,1)}, u32[]{:S(2)}) copy-start(bf16[3,384,256]{1,2,0:T(8,128)(2,1)} %copy-done.3) | copy-start | bytes 1769476 | tf_op jit(solution)/shard_map/while
  438.4 96.2 %copy-start.6 = (bf16[3,384,4,32]{1,3,2,0:T(8,128)(2,1)S(1)}, bf16[3,384,4,32]{1,3,2,0:T(8,128)(2,1)}, u32[]{:S(2)}) copy-start(bf16[3,384,4,32]{1,3,2,0:T(8,128)(2,1)} %copy-done.5) | copy-start | bytes 884740 | tf_op jit(solution)/shard_map/while
  438.5 96.2 %copy-start.8 = (bf16[3,384,4,32]{1,3,2,0:T(8,128)(2,1)S(1)}, bf16[3,384,4,32]{1,3,2,0:T(8,128)(2,1)}, u32[]{:S(2)}) copy-start(bf16[3,384,4,32]{1,3,2,0:T(8,128)(2,1)} %copy-done.7) | copy-start | bytes 884740 | tf_op jit(solution)/shard_map/while
  479.6 55.6 %collective-permute-start = (bf16[3,384,2048]{2,1,0:T(8,128)(2,1)}, bf16[3,384,2048]{2,1,0:T(8,128)(2,1)}, u32[]{:S(2)}, u32[]{:S(2)}) collective-permute-start(bf16[3,384,2048]{2,1,0:T(8,128)(2,1)} %fusion.255), channel_id=1, source_target_pairs={{0,1},{1,2},{2,3},{4,5},{5,6},{6,7},{8,9},{9,10},{10,11},{12,13},{... | collective-permute-start | bytes 14155784 | tf_op jit(solution)/shard_map/while/body/eval_jaxpr/ppermute | solution.py:147
  536.5 112.8 %copy-start.17 = (f32[1,2048]{1,0:T(1,128)}, f32[1,2048]{1,0:T(1,128)S(1)}, u32[]{:S(2)}) copy-start(f32[1,2048]{1,0:T(1,128)S(1)} %get-tuple-element.1275) | copy-start | bytes 24580 | tf_op jit(solution)/shard_map/while
  569.6 38.7 %copy-start.3 = (bf16[3,384,256]{1,2,0:T(8,128)(2,1)}, bf16[3,384,256]{1,2,0:T(8,128)(2,1)S(1)}, u32[]{:S(2)}) copy-start(bf16[3,384,256]{1,2,0:T(8,128)(2,1)S(1)} %copy.137) | copy-start | bytes 1769476 | tf_op jit(solution)/shard_map/while
  587.0 21.4 %copy-start.5 = (bf16[3,384,4,32]{1,3,2,0:T(8,128)(2,1)}, bf16[3,384,4,32]{1,3,2,0:T(8,128)(2,1)S(1)}, u32[]{:S(2)}) copy-start(bf16[3,384,4,32]{1,3,2,0:T(8,128)(2,1)S(1)} %get-tuple-element.1208) | copy-start | bytes 884740 | tf_op jit(solution)/shard_map/while
  587.0 21.4 %copy-start.7 = (bf16[3,384,4,32]{1,3,2,0:T(8,128)(2,1)}, bf16[3,384,4,32]{1,3,2,0:T(8,128)(2,1)S(1)}, u32[]{:S(2)}) copy-start(bf16[3,384,4,32]{1,3,2,0:T(8,128)(2,1)S(1)} %get-tuple-element.1207) | copy-start | bytes 884740 | tf_op jit(solution)/shard_map/while
  588.0 20.4 %copy-start.2 = (bf16[3,384,4,8,32]{1,4,3,2,0:T(8,128)(2,1)S(1)}, bf16[3,384,4,8,32]{1,4,3,2,0:T(8,128)(2,1)}, u32[]{:S(2)}) copy-start(bf16[3,384,4,8,32]{1,4,3,2,0:T(8,128)(2,1)} %get-tuple-element.1206) | copy-start | bytes 7077892 | tf_op jit(solution)/shard_map/while
  649.3 62.5 %copy-start.19 = (bf16[3,384,2048]{2,1,0:T(8,128)(2,1)}, bf16[3,384,2048]{2,1,0:T(8,128)(2,1)S(1)}, u32[]{:S(2)}) copy-start(bf16[3,384,2048]{2,1,0:T(8,128)(2,1)S(1)} %get-tuple-element.1209) | copy-start | bytes 14155780 | tf_op jit(solution)/shard_map/while
  711.7 96.0 %copy-start.9 = (bf16[1,6,384,4,64]{2,4,1,3,0:T(8,128)(2,1)S(1)}, bf16[1,6,384,4,64]{2,4,1,3,0:T(8,128)(2,1)}, u32[]{:S(2)}) copy-start(bf16[1,6,384,4,64]{2,4,1,3,0:T(8,128)(2,1)} %get-tuple-element.1241) | copy-start | bytes 3538948 | tf_op jit(solution)/shard_map/while
  711.8 96.0 %copy-start.11 = (bf16[1,6,384,4,64]{2,4,1,3,0:T(8,128)(2,1)S(1)}, bf16[1,6,384,4,64]{2,4,1,3,0:T(8,128)(2,1)}, u32[]{:S(2)}) copy-start(bf16[1,6,384,4,64]{2,4,1,3,0:T(8,128)(2,1)} %get-tuple-element.1240) | copy-start | bytes 3538948 | tf_op jit(solution)/shard_map/while
  711.8 96.1 %copy-start.4 = (bf16[3,384,256]{1,2,0:T(8,128)(2,1)S(1)}, bf16[3,384,256]{1,2,0:T(8,128)(2,1)}, u32[]{:S(2)}) copy-start(bf16[3,384,256]{1,2,0:T(8,128)(2,1)} %copy-done.3) | copy-start | bytes 1769476 | tf_op jit(solution)/shard_map/while
  711.8 96.1 %copy-start.6 = (bf16[3,384,4,32]{1,3,2,0:T(8,128)(2,1)S(1)}, bf16[3,384,4,32]{1,3,2,0:T(8,128)(2,1)}, u32[]{:S(2)}) copy-start(bf16[3,384,4,32]{1,3,2,0:T(8,128)(2,1)} %copy-done.5) | copy-start | bytes 884740 | tf_op jit(solution)/shard_map/while
  711.8 96.1 %copy-start.8 = (bf16[3,384,4,32]{1,3,2,0:T(8,128)(2,1)S(1)}, bf16[3,384,4,32]{1,3,2,0:T(8,128)(2,1)}, u32[]{:S(2)}) copy-start(bf16[3,384,4,32]{1,3,2,0:T(8,128)(2,1)} %copy-done.7) | copy-start | bytes 884740 | tf_op jit(solution)/shard_map/while
  752.9 55.5 %collective-permute-start = (bf16[3,384,2048]{2,1,0:T(8,128)(2,1)}, bf16[3,384,2048]{2,1,0:T(8,128)(2,1)}, u32[]{:S(2)}, u32[]{:S(2)}) collective-permute-start(bf16[3,384,2048]{2,1,0:T(8,128)(2,1)} %fusion.255), channel_id=1, source_target_pairs={{0,1},{1,2},{2,3},{4,5},{5,6},{6,7},{8,9},{9,10},{10,11},{12,13},{... | collective-permute-start | bytes 14155784 | tf_op jit(solution)/shard_map/while/body/eval_jaxpr/ppermute | solution.py:147
  809.8 112.8 %copy-start.17 = (f32[1,2048]{1,0:T(1,128)}, f32[1,2048]{1,0:T(1,128)S(1)}, u32[]{:S(2)}) copy-start(f32[1,2048]{1,0:T(1,128)S(1)} %get-tuple-element.1275) | copy-start | bytes 24580 | tf_op jit(solution)/shard_map/while
  842.9 38.7 %copy-start.3 = (bf16[3,384,256]{1,2,0:T(8,128)(2,1)}, bf16[3,384,256]{1,2,0:T(8,128)(2,1)S(1)}, u32[]{:S(2)}) copy-start(bf16[3,384,256]{1,2,0:T(8,128)(2,1)S(1)} %copy.137) | copy-start | bytes 1769476 | tf_op jit(solution)/shard_map/while
  860.2 21.4 %copy-start.5 = (bf16[3,384,4,32]{1,3,2,0:T(8,128)(2,1)}, bf16[3,384,4,32]{1,3,2,0:T(8,128)(2,1)S(1)}, u32[]{:S(2)}) copy-start(bf16[3,384,4,32]{1,3,2,0:T(8,128)(2,1)S(1)} %get-tuple-element.1208) | copy-start | bytes 884740 | tf_op jit(solution)/shard_map/while
  860.2 21.4 %copy-start.7 = (bf16[3,384,4,32]{1,3,2,0:T(8,128)(2,1)}, bf16[3,384,4,32]{1,3,2,0:T(8,128)(2,1)S(1)}, u32[]{:S(2)}) copy-start(bf16[3,384,4,32]{1,3,2,0:T(8,128)(2,1)S(1)} %get-tuple-element.1207) | copy-start | bytes 884740 | tf_op jit(solution)/shard_map/while
  861.2 20.4 %copy-start.2 = (bf16[3,384,4,8,32]{1,4,3,2,0:T(8,128)(2,1)S(1)}, bf16[3,384,4,8,32]{1,4,3,2,0:T(8,128)(2,1)}, u32[]{:S(2)}) copy-start(bf16[3,384,4,8,32]{1,4,3,2,0:T(8,128)(2,1)} %get-tuple-element.1206) | copy-start | bytes 7077892 | tf_op jit(solution)/shard_map/while
  922.5 62.5 %copy-start.19 = (bf16[3,384,2048]{2,1,0:T(8,128)(2,1)}, bf16[3,384,2048]{2,1,0:T(8,128)(2,1)S(1)}, u32[]{:S(2)}) copy-start(bf16[3,384,2048]{2,1,0:T(8,128)(2,1)S(1)} %get-tuple-element.1209) | copy-start | bytes 14155780 | tf_op jit(solution)/shard_map/while
  985.0 96.0 %copy-start.9 = (bf16[1,6,384,4,64]{2,4,1,3,0:T(8,128)(2,1)S(1)}, bf16[1,6,384,4,64]{2,4,1,3,0:T(8,128)(2,1)}, u32[]{:S(2)}) copy-start(bf16[1,6,384,4,64]{2,4,1,3,0:T(8,128)(2,1)} %get-tuple-element.1241) | copy-start | bytes 3538948 | tf_op jit(solution)/shard_map/while
  985.0 96.0 %copy-start.11 = (bf16[1,6,384,4,64]{2,4,1,3,0:T(8,128)(2,1)S(1)}, bf16[1,6,384,4,64]{2,4,1,3,0:T(8,128)(2,1)}, u32[]{:S(2)}) copy-start(bf16[1,6,384,4,64]{2,4,1,3,0:T(8,128)(2,1)} %get-tuple-element.1240) | copy-start | bytes 3538948 | tf_op jit(solution)/shard_map/while
  985.0 96.1 %copy-start.4 = (bf16[3,384,256]{1,2,0:T(8,128)(2,1)S(1)}, bf16[3,384,256]{1,2,0:T(8,128)(2,1)}, u32[]{:S(2)}) copy-start(bf16[3,384,256]{1,2,0:T(8,128)(2,1)} %copy-done.3) | copy-start | bytes 1769476 | tf_op jit(solution)/shard_map/while
  985.0 96.1 %copy-start.6 = (bf16[3,384,4,32]{1,3,2,0:T(8,128)(2,1)S(1)}, bf16[3,384,4,32]{1,3,2,0:T(8,128)(2,1)}, u32[]{:S(2)}) copy-start(bf16[3,384,4,32]{1,3,2,0:T(8,128)(2,1)} %copy-done.5) | copy-start | bytes 884740 | tf_op jit(solution)/shard_map/while
  985.0 96.1 %copy-start.8 = (bf16[3,384,4,32]{1,3,2,0:T(8,128)(2,1)S(1)}, bf16[3,384,4,32]{1,3,2,0:T(8,128)(2,1)}, u32[]{:S(2)}) copy-start(bf16[3,384,4,32]{1,3,2,0:T(8,128)(2,1)} %copy-done.7) | copy-start | bytes 884740 | tf_op jit(solution)/shard_map/while
  1026.1 55.5 %collective-permute-start = (bf16[3,384,2048]{2,1,0:T(8,128)(2,1)}, bf16[3,384,2048]{2,1,0:T(8,128)(2,1)}, u32[]{:S(2)}, u32[]{:S(2)}) collective-permute-start(bf16[3,384,2048]{2,1,0:T(8,128)(2,1)} %fusion.255), channel_id=1, source_target_pairs={{0,1},{1,2},{2,3},{4,5},{5,6},{6,7},{8,9},{9,10},{10,11},{12,13},{... | collective-permute-start | bytes 14155784 | tf_op jit(solution)/shard_map/while/body/eval_jaxpr/ppermute | solution.py:147
  1083.0 112.8 %copy-start.17 = (f32[1,2048]{1,0:T(1,128)}, f32[1,2048]{1,0:T(1,128)S(1)}, u32[]{:S(2)}) copy-start(f32[1,2048]{1,0:T(1,128)S(1)} %get-tuple-element.1275) | copy-start | bytes 24580 | tf_op jit(solution)/shard_map/while
  1116.1 38.7 %copy-start.3 = (bf16[3,384,256]{1,2,0:T(8,128)(2,1)}, bf16[3,384,256]{1,2,0:T(8,128)(2,1)S(1)}, u32[]{:S(2)}) copy-start(bf16[3,384,256]{1,2,0:T(8,128)(2,1)S(1)} %copy.137) | copy-start | bytes 1769476 | tf_op jit(solution)/shard_map/while
  1133.5 21.4 %copy-start.5 = (bf16[3,384,4,32]{1,3,2,0:T(8,128)(2,1)}, bf16[3,384,4,32]{1,3,2,0:T(8,128)(2,1)S(1)}, u32[]{:S(2)}) copy-start(bf16[3,384,4,32]{1,3,2,0:T(8,128)(2,1)S(1)} %get-tuple-element.1208) | copy-start | bytes 884740 | tf_op jit(solution)/shard_map/while
  1133.5 21.4 %copy-start.7 = (bf16[3,384,4,32]{1,3,2,0:T(8,128)(2,1)}, bf16[3,384,4,32]{1,3,2,0:T(8,128)(2,1)S(1)}, u32[]{:S(2)}) copy-start(bf16[3,384,4,32]{1,3,2,0:T(8,128)(2,1)S(1)} %get-tuple-element.1207) | copy-start | bytes 884740 | tf_op jit(solution)/shard_map/while
  1134.5 20.4 %copy-start.2 = (bf16[3,384,4,8,32]{1,4,3,2,0:T(8,128)(2,1)S(1)}, bf16[3,384,4,8,32]{1,4,3,2,0:T(8,128)(2,1)}, u32[]{:S(2)}) copy-start(bf16[3,384,4,8,32]{1,4,3,2,0:T(8,128)(2,1)} %get-tuple-element.1206) | copy-start | bytes 7077892 | tf_op jit(solution)/shard_map/while
  1195.8 62.5 %copy-start.19 = (bf16[3,384,2048]{2,1,0:T(8,128)(2,1)}, bf16[3,384,2048]{2,1,0:T(8,128)(2,1)S(1)}, u32[]{:S(2)}) copy-start(bf16[3,384,2048]{2,1,0:T(8,128)(2,1)S(1)} %get-tuple-element.1209) | copy-start | bytes 14155780 | tf_op jit(solution)/shard_map/while
  1258.2 96.0 %copy-start.9 = (bf16[1,6,384,4,64]{2,4,1,3,0:T(8,128)(2,1)S(1)}, bf16[1,6,384,4,64]{2,4,1,3,0:T(8,128)(2,1)}, u32[]{:S(2)}) copy-start(bf16[1,6,384,4,64]{2,4,1,3,0:T(8,128)(2,1)} %get-tuple-element.1241) | copy-start | bytes 3538948 | tf_op jit(solution)/shard_map/while
  1258.2 96.0 %copy-start.11 = (bf16[1,6,384,4,64]{2,4,1,3,0:T(8,128)(2,1)S(1)}, bf16[1,6,384,4,64]{2,4,1,3,0:T(8,128)(2,1)}, u32[]{:S(2)}) copy-start(bf16[1,6,384,4,64]{2,4,1,3,0:T(8,128)(2,1)} %get-tuple-element.1240) | copy-start | bytes 3538948 | tf_op jit(solution)/shard_map/while
  1258.2 96.1 %copy-start.4 = (bf16[3,384,256]{1,2,0:T(8,128)(2,1)S(1)}, bf16[3,384,256]{1,2,0:T(8,128)(2,1)}, u32[]{:S(2)}) copy-start(bf16[3,384,256]{1,2,0:T(8,128)(2,1)} %copy-done.3) | copy-start | bytes 1769476 | tf_op jit(solution)/shard_map/while
  1258.3 96.1 %copy-start.6 = (bf16[3,384,4,32]{1,3,2,0:T(8,128)(2,1)S(1)}, bf16[3,384,4,32]{1,3,2,0:T(8,128)(2,1)}, u32[]{:S(2)}) copy-start(bf16[3,384,4,32]{1,3,2,0:T(8,128)(2,1)} %copy-done.5) | copy-start | bytes 884740 | tf_op jit(solution)/shard_map/while
  1258.3 96.1 %copy-start.8 = (bf16[3,384,4,32]{1,3,2,0:T(8,128)(2,1)S(1)}, bf16[3,384,4,32]{1,3,2,0:T(8,128)(2,1)}, u32[]{:S(2)}) copy-start(bf16[3,384,4,32]{1,3,2,0:T(8,128)(2,1)} %copy-done.7) | copy-start | bytes 884740 | tf_op jit(solution)/shard_map/while
  1299.4 55.5 %collective-permute-start = (bf16[3,384,2048]{2,1,0:T(8,128)(2,1)}, bf16[3,384,2048]{2,1,0:T(8,128)(2,1)}, u32[]{:S(2)}, u32[]{:S(2)}) collective-permute-start(bf16[3,384,2048]{2,1,0:T(8,128)(2,1)} %fusion.255), channel_id=1, source_target_pairs={{0,1},{1,2},{2,3},{4,5},{5,6},{6,7},{8,9},{9,10},{10,11},{12,13},{... | collective-permute-start | bytes 14155784 | tf_op jit(solution)/shard_map/while/body/eval_jaxpr/ppermute | solution.py:147
  1359.5 67.5 %copy-start.16 = (bf16[6,2048]{1,0:T(8,128)(2,1)S(1)}, bf16[6,2048]{1,0:T(8,128)(2,1)}, u32[]{:S(2)}) copy-start(bf16[6,2048]{1,0:T(8,128)(2,1)} %get-tuple-element.519) | copy-start | bytes 73732
  1359.5 88.8 %copy-start.14 = (bf16[6,2048]{1,0:T(8,128)(2,1)S(1)}, bf16[6,2048]{1,0:T(8,128)(2,1)}, u32[]{:S(2)}) copy-start(bf16[6,2048]{1,0:T(8,128)(2,1)} %param.22) | copy-start | bytes 73732
  1422.6 25.6 %all-to-all-start = ((bf16[1,6,384,4,1,64]{2,5,1,4,0,3:T(8,128)(2,1)}), bf16[1,6,384,4,1,64]{2,5,1,4,0,3:T(8,128)(2,1)S(1)}, u32[]{:S(2)}, u32[]{:S(2)}) async-start(bf16[1,6,384,4,1,64]{2,5,1,4,0,3:T(8,128)(2,1)} %bitcast.308), calls=%async_computation | async-start | bytes 2359296 | tf_op jit(solution)/shard_map/all_to_all | solution.py:159
  (35 other events, 217.5 us)
where the time goes:
time: 1980 us
  matrix products  951 us (48%)
  blocking collectives  552 us (28%)
  starting transfers between devices  206 us (10%)
  local copies, waits for them, and re-layouts  133 us (7%)
  other arithmetic  103 us (5%)
  loops' own time  31.7 us (2%)
    dot_general x5, matrix products, stage_layer(): jnp.einsum('bsd,df->bsf', normed_mlp, w_gateup, preferred_element_type=jn...  312 us
    psum x4, blocking collectives, layer_fn(): lax.psum(jnp.einsum('bhe,hed->bd', attn_out, w_outp, preferred_element_ty...  236 us
    psum x4, blocking collectives, layer_fn(): lax.psum(jnp.dot(act_out, w_down, preferred_element_type=jnp.float32), TP...  232 us
    dot_general x5, matrix products, stage_layer(): jnp.einsum('bsf,df->bsd', act_out, w_down_t, preferred_element_type=jnp.f...  205 us
    ppermute x5, starting transfers between devices, tick_fn(): recv_act = lax.ppermute(hidden_x, 'model', send_pairs)  203 us
    dot_general x5, matrix products, stage_layer(): jnp.einsum('bcgqk,bkce->bqcge', probs_bf, val_proj, preferred_element_typ...  128 us
    sub x5, matrix products, stage_layer(): probs_bf = jax.nn.softmax(scores, axis=-1).astype(jnp.bfloat16)  102 us
    dot_general x5, matrix products, stage_layer(): jnp.einsum('bsd,df->bsf', normed, w_qkv, preferred_element_type=jnp.float32)  85.3 us
  transfers between devices with their start and end apart: 6, of which 0 were waited for; matrix products, arithmetic and copies ran while one was open for 2% of the time, Pallas kernels for 0%

commit v1 on v0

v1 whole, which is shorter than its diff:
```python
import jax
import jax.numpy as jnp
import numpy as np
from jax import lax
from jax.sharding import PartitionSpec as P

EPS = 1e-5
THETA = 10000.0
TP_AXES = ('model', 'model2')
NEG = -1e30

CHUNKS = (((4, 0), (1, 0), (5, 0), (3, 0)),
          ((0, 0), (1, 1), (2, 0), (3, 1)),
          ((0, 1), (4, 1), (2, 1), (5, 1)))


def rms_norm(values_in, gain_vec):
    x_f32 = values_in.astype(jnp.float32)
    inv_rms = lax.rsqrt(jnp.mean(x_f32 * x_f32, axis=-1, keepdims=True) + EPS)
    return (x_f32 * inv_rms * gain_vec).astype(jnp.bfloat16)


def rope_angles(positions, head_dim):
    half_dim = head_dim // 2
    inv_freq = jnp.power(THETA, jnp.arange(half_dim, dtype=jnp.float32) * (-2.0 / head_dim))
    angles = positions.astype(jnp.float32)[..., None] * inv_freq
    return jnp.cos(angles), jnp.sin(angles)


def apply_rope(values_in, cos_t, sin_t):
    half_dim = values_in.shape[-1] // 2
    first_half = values_in[..., :half_dim]
    second = values_in[..., half_dim:]
    return jnp.concatenate([first_half * cos_t - second * sin_t, second * cos_t + first_half * sin_t], axis=-1)


def dot32(a, b):
    return jnp.dot(a, b, preferred_element_type=jnp.float32)


def rope_flat(values_in, cos_t, sin_t, head_dim):
    rows, cols = values_in.shape
    v = values_in.reshape(rows, cols // head_dim, head_dim)
    return apply_rope(v, cos_t[:, None, :], sin_t[:, None, :]).astype(jnp.bfloat16).reshape(rows, cols)


def attend(q, keys, vals, mask, head_dim):
    rows = q.shape[0]
    kv_heads = keys.shape[1] // head_dim
    group = q.shape[1] // (kv_heads * head_dim)
    qh = q.reshape(rows, kv_heads, group, head_dim)
    kh = keys.reshape(-1, kv_heads, head_dim)
    vh = vals.reshape(-1, kv_heads, head_dim)
    scores = jnp.einsum('qcge,kce->cgqk', qh, kh, preferred_element_type=jnp.float32) * head_dim ** -0.5
    scores = jnp.where(mask[None, None], scores, NEG)
    probs = jax.nn.softmax(scores, axis=-1).astype(jnp.bfloat16)
    out = jnp.einsum('cgqk,kce->qcge', probs, vh, preferred_element_type=jnp.float32)
    return out.astype(jnp.bfloat16).reshape(rows, -1)


def finish(x, o, g_mlp, w_out, w_gateup, w_down_t):
    ff = w_down_t.shape[1]
    x1 = (x.astype(jnp.float32) + dot32(o, w_out)).astype(jnp.bfloat16)
    h2 = rms_norm(x1, g_mlp)
    gu = dot32(h2, w_gateup)
    act = (jax.nn.silu(gu[:, :ff]) * gu[:, ff:]).astype(jnp.bfloat16)
    down = lax.dot_general(act, w_down_t, (((1,), (1,)), ((), ())), preferred_element_type=jnp.float32)
    return (x1.astype(jnp.float32) + down).astype(jnp.bfloat16)


def solution(mesh):
    stages = mesh.shape['model']
    width = mesh.shape['model2']
    stage_spec = P('model', None, None)
    in_specs = (P('replica', None, None, None), P('replica', None), P('replica', None),
                stage_spec, stage_spec, stage_spec, stage_spec, P(None, None), P(None, None),
                P(None, None, TP_AXES, None), P(None, None, TP_AXES, None), P(None, None, TP_AXES, None),
                P(None, TP_AXES, None, None), P(None, None, TP_AXES), P(None, None, TP_AXES), P(None, TP_AXES, None))
    cache_spec = P(None, 'replica', None, TP_AXES, None)
    out_specs = (P('replica', None), P('replica', None), cache_spec, cache_spec)
    num_k = len(CHUNKS)
    pid_tab = np.array([[c[0] for c in row] for row in CHUNKS], np.int32)
    half_tab = np.array([[c[1] for c in row] for row in CHUNKS], np.int32)

    def shard_body(x_prompt, lengths, x_new, st_qkv, st_out, st_gateup, st_down_t, gain_attn, gain_mlp, tp_query, tp_key, tp_value, tp_out, tp_gate, tp_up, tp_down):
        seq_len, model_dim = x_prompt.shape[2:]
        batch = x_new.shape[0]
        head_dim = tp_query.shape[-1]
        w_qkv, w_out, w_gateup, w_down_t = st_qkv[0], st_out[0], st_gateup[0], st_down_t[0]
        q_cols = w_out.shape[0]
        k_cols = (w_qkv.shape[1] - q_cols) // 2
        kv_heads = k_cols // head_dim
        chunk = seq_len // 2
        rows = chunk + 16
        stage = lax.axis_index('model')
        col = lax.axis_index('model2')
        g_attn = lax.dynamic_index_in_dim(gain_attn, stage, 0, keepdims=False)
        g_mlp = lax.dynamic_index_in_dim(gain_mlp, stage, 0, keepdims=False)
        lens = lengths.reshape(batch)
        x_chunks = x_prompt.reshape(batch, 2, chunk, model_dim)
        pids = jnp.asarray(pid_tab)[:, col]
        halves = jnp.asarray(half_tab)[:, col]
        row_i = jnp.arange(rows)
        key_j = jnp.arange(chunk + rows)
        send_pairs = [(i, i + 1) for i in range(stages - 1)]
        pair_z = [(i, i + 1) for i in range(0, width, 2)]

        def fresh(k):
            body = x_chunks[pids[k], halves[k]]
            new_row = x_new[pids[k]]
            return jnp.concatenate([body, new_row[None], jnp.zeros((rows - chunk - 1, model_dim), jnp.bfloat16)], axis=0)

        def tick(carry, t):
            recv, prev_kv, nb_kv, kv_store, xsel, osel = carry
            k_raw = t - stage
            valid = (k_raw >= 0) & (k_raw < num_k)
            k = jnp.clip(k_raw, 0, num_k - 1)
            x = jnp.where(stage == 0, fresh(k), recv)
            length = lens[pids[k]]
            half = halves[k]
            pos = jnp.where(row_i < chunk, half * chunk + row_i, length)
            cos_t, sin_t = rope_angles(pos, head_dim)
            ctx = jnp.where((k == num_k - 1) & (col % 2 == 1), nb_kv, prev_kv)
            is_dec = row_i >= chunk
            own = key_j - chunk
            kpos = jnp.where(key_j < chunk, key_j, half * chunk + own)
            seen_ctx = (half == 1) & (key_j < chunk)
            seen_own = (own >= 0) & (own < chunk)
            mask = (seen_ctx | seen_own)[None] & (kpos[None] < length) & (is_dec[:, None] | (kpos[None] <= pos[:, None]))
            mask = mask | (is_dec[:, None] & (own == chunk)[None])

            def full(_):
                h = rms_norm(x, g_attn)
                qkv = dot32(h, w_qkv)
                q = rope_flat(qkv[:, :q_cols], cos_t, sin_t, head_dim)
                kk = rope_flat(qkv[:, q_cols:q_cols + k_cols], cos_t, sin_t, head_dim)
                vv = qkv[:, q_cols + k_cols:].astype(jnp.bfloat16)
                kv = jnp.concatenate([kk, vv], axis=1)
                allkv = jnp.concatenate([ctx, kv], axis=0)
                o = attend(q, allkv[:, :k_cols], allkv[:, k_cols:], mask, head_dim)
                y = finish(x, o, g_mlp, w_out, w_gateup, w_down_t)
                return y, kv, jnp.zeros((16, model_dim), jnp.bfloat16), jnp.zeros((16, q_cols), jnp.bfloat16)

            def light(_):
                h = rms_norm(x, g_attn)
                kvp = dot32(h, w_qkv[:, q_cols:])
                kk = rope_flat(kvp[:, :k_cols], cos_t, sin_t, head_dim)
                kv = jnp.concatenate([kk, kvp[:, k_cols:].astype(jnp.bfloat16)], axis=1)
                allkv = jnp.concatenate([ctx, kv], axis=0)
                last_i = jnp.clip(length - 1 - half * chunk, 0, chunk - 1)
                sel = jnp.where(jnp.arange(16) == 0, last_i, chunk)
                hs = h[sel]
                q = rope_flat(dot32(hs, w_qkv[:, :q_cols]), cos_t[sel], sin_t[sel], head_dim)
                o = attend(q, allkv[:, :k_cols], allkv[:, k_cols:], mask[sel], head_dim)
                return x, kv, x[sel], o

            y, kv, xs, osx = lax.cond(stage == stages - 1, light, full, None)
            recv = lax.ppermute(y, 'model', send_pairs)
            nb_new = lax.ppermute(kv[:chunk], 'model2', pair_z)
            nb_kv = jnp.where(k_raw == 0, nb_new, nb_kv)
            upd = lambda store, new: lax.dynamic_update_index_in_dim(store, jnp.where(valid, new, lax.dynamic_index_in_dim(store, k, 0, keepdims=False)), k, 0)
            return (recv, kv[:chunk], nb_kv, upd(kv_store, kv), upd(xsel, xs), upd(osel, osx)), None

        zkv = jnp.zeros((chunk, 2 * k_cols), jnp.bfloat16)
        init = (jnp.zeros((rows, model_dim), jnp.bfloat16), zkv, zkv,
                jnp.zeros((num_k, rows, 2 * k_cols), jnp.bfloat16),
                jnp.zeros((num_k, 16, model_dim), jnp.bfloat16), jnp.zeros((num_k, 16, q_cols), jnp.bfloat16))
        final = lax.scan(tick, init, jnp.arange(num_k + stages - 1))[0]
        _, _, _, kv_store, xsel, osel = final

        x6 = xsel[:, :2].reshape(2 * num_k, model_dim)
        o6 = osel[:, :2].reshape(2 * num_k, q_cols)
        y6 = lax.cond(stage == stages - 1, lambda: finish(x6, o6, g_mlp, w_out, w_gateup, w_down_t), lambda: x6)
        rows_all = lax.all_gather(y6, TP_AXES)[(stages - 1) * width:]
        rows_all = rows_all.reshape(width, num_k, 2, model_dim)
        where_a = {}
        where_b = {}
        for k in range(num_k):
            for z in range(width):
                (where_b if CHUNKS[k][z][1] else where_a)[CHUNKS[k][z][0]] = (z, k)
        dec = jnp.stack([rows_all[where_b[p] + (1,)] for p in range(batch)])
        last = jnp.stack([jnp.where(lens[p] > chunk, rows_all[where_b[p] + (0,)], rows_all[where_a[p] + (0,)]) for p in range(batch)])

        packed = jnp.stack([jnp.concatenate([kv_store[:, :, h * head_dim:(h + 1) * head_dim],
                                             kv_store[:, :, k_cols + h * head_dim:k_cols + (h + 1) * head_dim]], axis=-1)
                            for h in range(kv_heads)])
        moved = lax.all_to_all(packed, 'model', 0, 0, tiled=True)
        spread = lax.all_gather(moved, 'model2')
        full_kv = jnp.stack([jnp.concatenate([spread[where_a[p][0], :, where_a[p][1], :chunk],
                                              spread[where_b[p][0], :, where_b[p][1], :chunk + 1]], axis=1)
                             for p in range(batch)], axis=1)
        k_full = full_kv[:, :, :, None, :head_dim]
        v_full = full_kv[:, :, :, None, head_dim:]
        return dec, last, k_full, v_full

    return jax.shard_map(shard_body, mesh=mesh, in_specs=in_specs, out_specs=out_specs, check_vma=False)
```

time: 1980 us -> 785 us (0.40)
  matrix products: 951 us -> 388 us
  blocking collectives: 552 us -> 90.1 us
  starting transfers between devices: 206 us -> 45.4 us
  other arithmetic: 103 us -> 68.7 us
    dot_general x61 -> x30, matrix products: 849 us -> 325 us  [the longest x18 198 us: dot32(): return jnp.dot(a, b, preferred_element_type=jnp.float32)]
    psum x9 -> x0, blocking collectives: 489 us -> none  [the longest x4 236 us: layer_fn(): lax.psum(jnp.einsum('bhe,hed->bd', attn_out, w_outp, preferred_element_ty...]
    ppermute x5 -> x12, starting transfers between devices: 203 us -> 45.4 us  [the longest x6 24.7 us: tick(): recv = lax.ppermute(y, 'model', send_pairs)]
    all_gather x0 -> x1, blocking collectives: none -> 73.7 us  [shard_body(): rows_all = lax.all_gather(y6, TP_AXES)[(stages - 1) * width:]]
    all_to_all x1, blocking collectives: 63.2 us -> 16.5 us  [shard_body(): moved = lax.all_to_all(packed, 'model', 0, 0, tiled=True)]
    sub x5 -> x6, matrix products: 102 us -> 62.7 us  [attend(): probs = jax.nn.softmax(scores, axis=-1).astype(jnp.bfloat16)]
    dynamic_slice x24 -> x49, local copies, waits for them, and re-layouts: 14.2 us -> 43.6 us  [the longest x18 15.8 us: tick(): lax.dynamic_index_in_dim(store, k, 0, keepdims=False)]
    reduce_sum x13 -> x6, other arithmetic: 24.1 us -> 1.49 us  [rms_norm(): inv_rms = lax.rsqrt(jnp.mean(x_f32 * x_f32, axis=-1, keepdims=True) + EPS)]
  transfers between devices with their start and end apart: 6 -> 13, of which waited for: 0 -> 0; matrix products, arithmetic and copies ran while one was open for 2% -> 5% of each run, Pallas kernels for 0% -> 0%
where the time goes in v1:
time: 785 us; the launch traced here: 780 us
  matrix products  388 us (49%)
  local copies, waits for them, and re-layouts  134 us (17%)
  blocking collectives  90.1 us (11%)
  other arithmetic  68.7 us (9%)
  starting transfers between devices  45.4 us (6%)
  loops' own time  35.9 us (5%)
  between operations  18 us (2%)
    dot_general x18, matrix products, dot32(): return jnp.dot(a, b, preferred_element_type=jnp.float32)  198 us
    dot_general x6, matrix products, finish(): lax.dot_general(act, w_down_t, (((1,), (1,)), ((), ())), preferred_elemen...  90.6 us
    all_gather x1, blocking collectives, shard_body(): rows_all = lax.all_gather(y6, TP_AXES)[(stages - 1) * width:]  73.7 us
    sub x6, matrix products, attend(): probs = jax.nn.softmax(scores, axis=-1).astype(jnp.bfloat16)  62.7 us
    dot_general x6, matrix products, attend(): jnp.einsum('cgqk,kce->qcge', probs, vh, preferred_element_type=jnp.float32)  36.1 us
    another operation x1, loops' own time, shard_body(): final = lax.scan(tick, init, jnp.arange(num_k + stages - 1))[0]  35.2 us
    ppermute x6, starting transfers between devices, tick(): recv = lax.ppermute(y, 'model', send_pairs)  24.7 us
    ppermute x6, starting transfers between devices, tick(): nb_new = lax.ppermute(kv[:chunk], 'model2', pair_z)  20.7 us
  transfers between devices with their start and end apart: 13, of which 0 were waited for; matrix products, arithmetic and copies ran while one was open for 5% of the time, Pallas kernels for 0%

profile of v1, /device:TPU:0, one launch (start us, length us, event | category | flops | bytes accessed | tf_op | source)
XLA Modules:
  0.0 780.0 jit_solution(14720166451603093257)
XLA Ops:
  13.7 648.0 %while.24 = (s32[]{:T(128)}, bf16[208,2048]{1,0:T(8,128)(2,1)S(1)}, bf16[192,512]{1,0:T(8,128)(2,1)}, bf16[192,512]{1,0:T(8,128)(2,1)}, bf16[3,208,512]{2,1,0:T(...) while((s32[]{:T(128)}, bf16[208,2048]{1,0:T(8,128)(2,1)S(1)}, ...), condition=%wide.region_10.11_spmd.clone.clone, body=%wide.region_0.10_spmd.clone.clone.sunk | while | flops 19044104192 | bytes 167009168 | solution.py:168
  29.8 78.3 %conditional.6 = (bf16[208,2048]{1,0:T(8,128)(2,1)}, bf16[208,512]{1,0:T(8,128)(2,1)S(1)}, bf16[16,2048]{1,0:T(8,128)(2,1)}, bf16[16,2048]{1,0:T(8,128)(2,1)}, bf16[192,512]{1,0:T(8,128)(2,1)}) conditional(s32[]{:T(128)} %convert_element_type.207, (bf16[208,2048]{1,0:T(8,128)(2,1)S(1)}, f32[2048]{0:T(1024)S(1)}, ...), branch_computations={%region_1.5_spmd.clone, %region_6.9_spmd.clone} | conditional | flops 19040124928 | bytes 155692448 | solution.py:157
  30.0 6.4 fusion.36
  44.2 1.9 copy.64
  47.6 10.5 %fusion.116 = (f32[4,8,208]{2,1,0:T(8,128)S(1)}, f32[4,8,208,400]{2,3,1,0:T(8,128)}) fusion(pred[208,400]{0,1:T(8,128)(4,1)S(1)} %copy.76, bf16[400,4,64,1]{0,2,3,1:T(8,128)(2,1)} %bitcast.262, bf16[208,4,8,32]{0,3,2,1:T(8,128)(2,1)} %bitcast.257, bf16[208,4,8,32]{0,3,2,1:T(8,128)(2,1)} %bitcast.256), kind=kOutput, calls=%fused_computation.212 | convolution fusion | flops 353141120 | bytes 11816192 | tf_op jit(solution)/shard_map/while/body/eval_jaxpr/cond/branch_0_fun/sub | solution.py:56
  58.2 6.0 fusion.31
  64.3 5.5 fusion.28
  69.8 21.2 %fusion.34 = f32[208,11264]{1,0:T(8,128)} fusion(bf16[2048,11264]{1,0:T(8,128)(2,1)} %get-tuple-element.475, bf16[208,2048]{1,0:T(8,128)(2,1)S(1)} %get-tuple-element.740, f32[2048]{0:T(1024)S(1)} %get-tuple-element.474, f32[208]{0:T(256)S(1)} %add_rsqrt_fusion.1), kind=kOutput, calls=%fused_computation.53 | convolution fusion | flops 9598271488 | bytes 56369984 | tf_op jit(solution)/shard_map/while/body/eval_jaxpr/cond/branch_0_fun/dot_general | solution.py:38
  91.0 15.1 %fusion.22 = bf16[208,2048]{1,0:T(8,128)(2,1)} fusion(bf16[2048,5632]{1,0:T(8,128)(2,1)} %get-tuple-element.476, bf16[208,2048]{1,0:T(8,128)(2,1)S(1)} %get-tuple-element.740, f32[208,11264]{1,0:T(8,128)} %fusion.34), kind=kOutput, calls=%fused_computation.40 | convolution fusion | flops 4806590464 | bytes 34144256 | tf_op jit(solution)/shard_map/while/body/eval_jaxpr/cond/branch_0_fun/dot_general | solution.py:67
  108.0 2.5 collective-permute-start
  110.5 4.3 collective-permute-start.1
  136.6 78.3 %conditional.6 = (bf16[208,2048]{1,0:T(8,128)(2,1)}, bf16[208,512]{1,0:T(8,128)(2,1)S(1)}, bf16[16,2048]{1,0:T(8,128)(2,1)}, bf16[16,2048]{1,0:T(8,128)(2,1)}, bf16[192,512]{1,0:T(8,128)(2,1)}) conditional(s32[]{:T(128)} %convert_element_type.207, (bf16[208,2048]{1,0:T(8,128)(2,1)S(1)}, f32[2048]{0:T(1024)S(1)}, ...), branch_computations={%region_1.5_spmd.clone, %region_6.9_spmd.clone} | conditional | flops 19040124928 | bytes 155692448 | solution.py:157
  136.9 6.4 fusion.36
  151.1 1.9 copy.64
  154.5 10.5 %fusion.116 = (f32[4,8,208]{2,1,0:T(8,128)S(1)}, f32[4,8,208,400]{2,3,1,0:T(8,128)}) fusion(pred[208,400]{0,1:T(8,128)(4,1)S(1)} %copy.76, bf16[400,4,64,1]{0,2,3,1:T(8,128)(2,1)} %bitcast.262, bf16[208,4,8,32]{0,3,2,1:T(8,128)(2,1)} %bitcast.257, bf16[208,4,8,32]{0,3,2,1:T(8,128)(2,1)} %bitcast.256), kind=kOutput, calls=%fused_computation.212 | convolution fusion | flops 353141120 | bytes 11816192 | tf_op jit(solution)/shard_map/while/body/eval_jaxpr/cond/branch_0_fun/sub | solution.py:56
  165.1 6.0 fusion.31
  171.1 5.5 fusion.28
  176.7 21.2 %fusion.34 = f32[208,11264]{1,0:T(8,128)} fusion(bf16[2048,11264]{1,0:T(8,128)(2,1)} %get-tuple-element.475, bf16[208,2048]{1,0:T(8,128)(2,1)S(1)} %get-tuple-element.740, f32[2048]{0:T(1024)S(1)} %get-tuple-element.474, f32[208]{0:T(256)S(1)} %add_rsqrt_fusion.1), kind=kOutput, calls=%fused_computation.53 | convolution fusion | flops 9598271488 | bytes 56369984 | tf_op jit(solution)/shard_map/while/body/eval_jaxpr/cond/branch_0_fun/dot_general | solution.py:38
  197.8 15.1 %fusion.22 = bf16[208,2048]{1,0:T(8,128)(2,1)} fusion(bf16[2048,5632]{1,0:T(8,128)(2,1)} %get-tuple-element.476, bf16[208,2048]{1,0:T(8,128)(2,1)S(1)} %get-tuple-element.740, f32[208,11264]{1,0:T(8,128)} %fusion.34), kind=kOutput, calls=%fused_computation.40 | convolution fusion | flops 4806590464 | bytes 34144256 | tf_op jit(solution)/shard_map/while/body/eval_jaxpr/cond/branch_0_fun/dot_general | solution.py:67
  214.9 4.1 collective-permute-start
  219.0 3.5 collective-permute-start.1
  245.3 78.2 %conditional.6 = (bf16[208,2048]{1,0:T(8,128)(2,1)}, bf16[208,512]{1,0:T(8,128)(2,1)S(1)}, bf16[16,2048]{1,0:T(8,128)(2,1)}, bf16[16,2048]{1,0:T(8,128)(2,1)}, bf16[192,512]{1,0:T(8,128)(2,1)}) conditional(s32[]{:T(128)} %convert_element_type.207, (bf16[208,2048]{1,0:T(8,128)(2,1)S(1)}, f32[2048]{0:T(1024)S(1)}, ...), branch_computations={%region_1.5_spmd.clone, %region_6.9_spmd.clone} | conditional | flops 19040124928 | bytes 155692448 | solution.py:157
  245.5 6.4 fusion.36
  259.7 1.9 copy.64
  263.1 10.4 %fusion.116 = (f32[4,8,208]{2,1,0:T(8,128)S(1)}, f32[4,8,208,400]{2,3,1,0:T(8,128)}) fusion(pred[208,400]{0,1:T(8,128)(4,1)S(1)} %copy.76, bf16[400,4,64,1]{0,2,3,1:T(8,128)(2,1)} %bitcast.262, bf16[208,4,8,32]{0,3,2,1:T(8,128)(2,1)} %bitcast.257, bf16[208,4,8,32]{0,3,2,1:T(8,128)(2,1)} %bitcast.256), kind=kOutput, calls=%fused_computation.212 | convolution fusion | flops 353141120 | bytes 11816192 | tf_op jit(solution)/shard_map/while/body/eval_jaxpr/cond/branch_0_fun/sub | solution.py:56
  273.7 6.0 fusion.31
  279.7 5.5 fusion.28
  285.3 21.2 %fusion.34 = f32[208,11264]{1,0:T(8,128)} fusion(bf16[2048,11264]{1,0:T(8,128)(2,1)} %get-tuple-element.475, bf16[208,2048]{1,0:T(8,128)(2,1)S(1)} %get-tuple-element.740, f32[2048]{0:T(1024)S(1)} %get-tuple-element.474, f32[208]{0:T(256)S(1)} %add_rsqrt_fusion.1), kind=kOutput, calls=%fused_computation.53 | convolution fusion | flops 9598271488 | bytes 56369984 | tf_op jit(solution)/shard_map/while/body/eval_jaxpr/cond/branch_0_fun/dot_general | solution.py:38
  306.4 15.1 %fusion.22 = bf16[208,2048]{1,0:T(8,128)(2,1)} fusion(bf16[2048,5632]{1,0:T(8,128)(2,1)} %get-tuple-element.476, bf16[208,2048]{1,0:T(8,128)(2,1)S(1)} %get-tuple-element.740, f32[208,11264]{1,0:T(8,128)} %fusion.34), kind=kOutput, calls=%fused_computation.40 | convolution fusion | flops 4806590464 | bytes 34144256 | tf_op jit(solution)/shard_map/while/body/eval_jaxpr/cond/branch_0_fun/dot_general | solution.py:67
  323.5 4.1 collective-permute-start
  327.7 3.2 collective-permute-start.1
  353.7 78.3 %conditional.6 = (bf16[208,2048]{1,0:T(8,128)(2,1)}, bf16[208,512]{1,0:T(8,128)(2,1)S(1)}, bf16[16,2048]{1,0:T(8,128)(2,1)}, bf16[16,2048]{1,0:T(8,128)(2,1)}, bf16[192,512]{1,0:T(8,128)(2,1)}) conditional(s32[]{:T(128)} %convert_element_type.207, (bf16[208,2048]{1,0:T(8,128)(2,1)S(1)}, f32[2048]{0:T(1024)S(1)}, ...), branch_computations={%region_1.5_spmd.clone, %region_6.9_spmd.clone} | conditional | flops 19040124928 | bytes 155692448 | solution.py:157
  354.0 6.4 fusion.36
  368.1 1.9 copy.64
  371.6 10.4 %fusion.116 = (f32[4,8,208]{2,1,0:T(8,128)S(1)}, f32[4,8,208,400]{2,3,1,0:T(8,128)}) fusion(pred[208,400]{0,1:T(8,128)(4,1)S(1)} %copy.76, bf16[400,4,64,1]{0,2,3,1:T(8,128)(2,1)} %bitcast.262, bf16[208,4,8,32]{0,3,2,1:T(8,128)(2,1)} %bitcast.257, bf16[208,4,8,32]{0,3,2,1:T(8,128)(2,1)} %bitcast.256), kind=kOutput, calls=%fused_computation.212 | convolution fusion | flops 353141120 | bytes 11816192 | tf_op jit(solution)/shard_map/while/body/eval_jaxpr/cond/branch_0_fun/sub | solution.py:56
  382.2 6.0 fusion.31
  388.2 5.5 fusion.28
  393.7 21.2 %fusion.34 = f32[208,11264]{1,0:T(8,128)} fusion(bf16[2048,11264]{1,0:T(8,128)(2,1)} %get-tuple-element.475, bf16[208,2048]{1,0:T(8,128)(2,1)S(1)} %get-tuple-element.740, f32[2048]{0:T(1024)S(1)} %get-tuple-element.474, f32[208]{0:T(256)S(1)} %add_rsqrt_fusion.1), kind=kOutput, calls=%fused_computation.53 | convolution fusion | flops 9598271488 | bytes 56369984 | tf_op jit(solution)/shard_map/while/body/eval_jaxpr/cond/branch_0_fun/dot_general | solution.py:38
  414.9 15.1 %fusion.22 = bf16[208,2048]{1,0:T(8,128)(2,1)} fusion(bf16[2048,5632]{1,0:T(8,128)(2,1)} %get-tuple-element.476, bf16[208,2048]{1,0:T(8,128)(2,1)S(1)} %get-tuple-element.740, f32[208,11264]{1,0:T(8,128)} %fusion.34), kind=kOutput, calls=%fused_computation.40 | convolution fusion | flops 4806590464 | bytes 34144256 | tf_op jit(solution)/shard_map/while/body/eval_jaxpr/cond/branch_0_fun/dot_general | solution.py:67
  432.0 4.1 collective-permute-start
  436.0 3.2 collective-permute-start.1
  461.1 78.2 %conditional.6 = (bf16[208,2048]{1,0:T(8,128)(2,1)}, bf16[208,512]{1,0:T(8,128)(2,1)S(1)}, bf16[16,2048]{1,0:T(8,128)(2,1)}, bf16[16,2048]{1,0:T(8,128)(2,1)}, bf16[192,512]{1,0:T(8,128)(2,1)}) conditional(s32[]{:T(128)} %convert_element_type.207, (bf16[208,2048]{1,0:T(8,128)(2,1)S(1)}, f32[2048]{0:T(1024)S(1)}, ...), branch_computations={%region_1.5_spmd.clone, %region_6.9_spmd.clone} | conditional | flops 19040124928 | bytes 155692448 | solution.py:157
  461.4 6.4 fusion.36
  479.0 10.4 %fusion.116 = (f32[4,8,208]{2,1,0:T(8,128)S(1)}, f32[4,8,208,400]{2,3,1,0:T(8,128)}) fusion(pred[208,400]{0,1:T(8,128)(4,1)S(1)} %copy.76, bf16[400,4,64,1]{0,2,3,1:T(8,128)(2,1)} %bitcast.262, bf16[208,4,8,32]{0,3,2,1:T(8,128)(2,1)} %bitcast.257, bf16[208,4,8,32]{0,3,2,1:T(8,128)(2,1)} %bitcast.256), kind=kOutput, calls=%fused_computation.212 | convolution fusion | flops 353141120 | bytes 11816192 | tf_op jit(solution)/shard_map/while/body/eval_jaxpr/cond/branch_0_fun/sub | solution.py:56
  489.6 6.0 fusion.31
  495.6 5.5 fusion.28
  501.2 21.2 %fusion.34 = f32[208,11264]{1,0:T(8,128)} fusion(bf16[2048,11264]{1,0:T(8,128)(2,1)} %get-tuple-element.475, bf16[208,2048]{1,0:T(8,128)(2,1)S(1)} %get-tuple-element.740, f32[2048]{0:T(1024)S(1)} %get-tuple-element.474, f32[208]{0:T(256)S(1)} %add_rsqrt_fusion.1), kind=kOutput, calls=%fused_computation.53 | convolution fusion | flops 9598271488 | bytes 56369984 | tf_op jit(solution)/shard_map/while/body/eval_jaxpr/cond/branch_0_fun/dot_general | solution.py:38
  522.3 15.1 %fusion.22 = bf16[208,2048]{1,0:T(8,128)(2,1)} fusion(bf16[2048,5632]{1,0:T(8,128)(2,1)} %get-tuple-element.476, bf16[208,2048]{1,0:T(8,128)(2,1)S(1)} %get-tuple-element.740, f32[208,11264]{1,0:T(8,128)} %fusion.34), kind=kOutput, calls=%fused_computation.40 | convolution fusion | flops 4806590464 | bytes 34144256 | tf_op jit(solution)/shard_map/while/body/eval_jaxpr/cond/branch_0_fun/dot_general | solution.py:67
  539.4 5.1 collective-permute-start
  544.5 3.1 collective-permute-start.1
  569.5 78.2 %conditional.6 = (bf16[208,2048]{1,0:T(8,128)(2,1)}, bf16[208,512]{1,0:T(8,128)(2,1)S(1)}, bf16[16,2048]{1,0:T(8,128)(2,1)}, bf16[16,2048]{1,0:T(8,128)(2,1)}, bf16[192,512]{1,0:T(8,128)(2,1)}) conditional(s32[]{:T(128)} %convert_element_type.207, (bf16[208,2048]{1,0:T(8,128)(2,1)S(1)}, f32[2048]{0:T(1024)S(1)}, ...), branch_computations={%region_1.5_spmd.clone, %region_6.9_spmd.clone} | conditional | flops 19040124928 | bytes 155692448 | solution.py:157
  569.8 6.4 fusion.36
  587.4 10.4 %fusion.116 = (f32[4,8,208]{2,1,0:T(8,128)S(1)}, f32[4,8,208,400]{2,3,1,0:T(8,128)}) fusion(pred[208,400]{0,1:T(8,128)(4,1)S(1)} %copy.76, bf16[400,4,64,1]{0,2,3,1:T(8,128)(2,1)} %bitcast.262, bf16[208,4,8,32]{0,3,2,1:T(8,128)(2,1)} %bitcast.257, bf16[208,4,8,32]{0,3,2,1:T(8,128)(2,1)} %bitcast.256), kind=kOutput, calls=%fused_computation.212 | convolution fusion | flops 353141120 | bytes 11816192 | tf_op jit(solution)/shard_map/while/body/eval_jaxpr/cond/branch_0_fun/sub | solution.py:56
  598.0 6.0 fusion.31
  604.0 5.5 fusion.28
  609.6 21.2 %fusion.34 = f32[208,11264]{1,0:T(8,128)} fusion(bf16[2048,11264]{1,0:T(8,128)(2,1)} %get-tuple-element.475, bf16[208,2048]{1,0:T(8,128)(2,1)S(1)} %get-tuple-element.740, f32[2048]{0:T(1024)S(1)} %get-tuple-element.474, f32[208]{0:T(256)S(1)} %add_rsqrt_fusion.1), kind=kOutput, calls=%fused_computation.53 | convolution fusion | flops 9598271488 | bytes 56369984 | tf_op jit(solution)/shard_map/while/body/eval_jaxpr/cond/branch_0_fun/dot_general | solution.py:38
  630.7 15.1 %fusion.22 = bf16[208,2048]{1,0:T(8,128)(2,1)} fusion(bf16[2048,5632]{1,0:T(8,128)(2,1)} %get-tuple-element.476, bf16[208,2048]{1,0:T(8,128)(2,1)S(1)} %get-tuple-element.740, f32[208,11264]{1,0:T(8,128)} %fusion.34), kind=kOutput, calls=%fused_computation.40 | convolution fusion | flops 4806590464 | bytes 34144256 | tf_op jit(solution)/shard_map/while/body/eval_jaxpr/cond/branch_0_fun/dot_general | solution.py:67
  647.8 4.8 collective-permute-start
  652.6 3.3 collective-permute-start.1
  663.9 16.5 %all_to_all.5 = bf16[4,3,208,128]{3,2,1,0:T(8,128)(2,1)} all-to-all(bf16[4,3,208,128]{3,2,1,0:T(8,128)(2,1)S(1)} %pad_maximum_fusion.11), channel_id=1, replica_groups=mesh['replica'=2,'model2'=4,'model'=4] {'model'}, dimensions={0} | all-to-all | bytes 1277952 | tf_op jit(solution)/shard_map/all_to_all | solution.py:187
  681.4 73.7 %all-gather.2 = bf16[16,6,2048]{2,1,0:T(8,128)(2,1)S(1)} all-gather(bf16[1,6,2048]{2,1,0:T(8,128)(2,1)S(1)} %bitcast.275), channel_id=2, replica_groups=mesh['replica'=2,'model2'=4,'model'=4] {'model','model2'}, dimensions={0}, use_global_device_ids=true | all-gather | bytes 417792 | tf_op jit(solution)/shard_map/all_gather | solution.py:174
  764.4 2.3 slice_bitcast_fusion
  766.7 4.1 copy.89
  770.8 2.4 copy.90
  (381 shorter events, 186.5 us)
Async XLA Ops:
  7.2 754.0 %all-gather.5.cloned.1.call-start = ((), (), s32[]{:S(2)}) async-start(), calls=%async_computation.1 | async-start | bytes 3194880 | tf_op jit(solution)/shard_map/all_gather | solution.py:188
  39.0 1.1 copy-start.3
  44.2 1.9 copy-start.4
  46.0 1.4 copy-start.1
  47.6 10.5 %copy-start = (bf16[400,256]{1,0:T(8,128)(2,1)S(1)}, bf16[400,256]{1,0:T(8,128)(2,1)}, u32[]{:S(2)}) copy-start(bf16[400,256]{1,0:T(8,128)(2,1)} %get-tuple-element.734) | copy-start | bytes 614404 | tf_op jit(solution)/shard_map/while/body/eval_jaxpr/cond
  108.0 12.5 %collective-permute-start = (bf16[208,2048]{1,0:T(8,128)(2,1)}, bf16[208,2048]{1,0:T(8,128)(2,1)S(1)}, u32[]{:S(2)}, u32[]{:S(2)}) collective-permute-start(bf16[208,2048]{1,0:T(8,128)(2,1)} %get-tuple-element.945), channel_id=1, source_target_pairs={{0,1},{1,2},{2,3},{4,5},{5,6},{6,7},{8,9},{9,10},{10,11},{12,13},{... | collective-permute-start | bytes 2555912 | tf_op jit(solution)/shard_map/while/body/eval_jaxpr/ppermute | solution.py:158
  110.5 9.3 %collective-permute-start.1 = (bf16[192,512]{1,0:T(8,128)(2,1)}, bf16[192,512]{1,0:T(8,128)(2,1)S(1)}, u32[]{:S(2)}, u32[]{:S(2)}) collective-permute-start(bf16[192,512]{1,0:T(8,128)(2,1)} %get-tuple-element.1026), channel_id=1, source_target_pairs={{0,4},{8,12},{1,5},{9,13},{2,6},{10,14},{3,7},{11,15},{16,20},{24,... | collective-permute-start | bytes 589832 | tf_op jit(solution)/shard_map/while/body/eval_jaxpr/ppermute | solution.py:159
  145.9 1.1 copy-start.3
  151.1 1.9 copy-start.4
  152.9 1.4 copy-start.1
  154.5 10.5 %copy-start = (bf16[400,256]{1,0:T(8,128)(2,1)S(1)}, bf16[400,256]{1,0:T(8,128)(2,1)}, u32[]{:S(2)}) copy-start(bf16[400,256]{1,0:T(8,128)(2,1)} %get-tuple-element.734) | copy-start | bytes 614404 | tf_op jit(solution)/shard_map/while/body/eval_jaxpr/cond
  214.9 14.2 %collective-permute-start = (bf16[208,2048]{1,0:T(8,128)(2,1)}, bf16[208,2048]{1,0:T(8,128)(2,1)S(1)}, u32[]{:S(2)}, u32[]{:S(2)}) collective-permute-start(bf16[208,2048]{1,0:T(8,128)(2,1)} %get-tuple-element.945), channel_id=1, source_target_pairs={{0,1},{1,2},{2,3},{4,5},{5,6},{6,7},{8,9},{9,10},{10,11},{12,13},{... | collective-permute-start | bytes 2555912 | tf_op jit(solution)/shard_map/while/body/eval_jaxpr/ppermute | solution.py:158
  219.0 8.4 %collective-permute-start.1 = (bf16[192,512]{1,0:T(8,128)(2,1)}, bf16[192,512]{1,0:T(8,128)(2,1)S(1)}, u32[]{:S(2)}, u32[]{:S(2)}) collective-permute-start(bf16[192,512]{1,0:T(8,128)(2,1)} %get-tuple-element.1026), channel_id=1, source_target_pairs={{0,4},{8,12},{1,5},{9,13},{2,6},{10,14},{3,7},{11,15},{16,20},{24,... | collective-permute-start | bytes 589832 | tf_op jit(solution)/shard_map/while/body/eval_jaxpr/ppermute | solution.py:159
  254.5 1.1 copy-start.3
  259.7 1.9 copy-start.4
  261.5 1.4 copy-start.1
  263.1 10.5 %copy-start = (bf16[400,256]{1,0:T(8,128)(2,1)S(1)}, bf16[400,256]{1,0:T(8,128)(2,1)}, u32[]{:S(2)}) copy-start(bf16[400,256]{1,0:T(8,128)(2,1)} %get-tuple-element.734) | copy-start | bytes 614404 | tf_op jit(solution)/shard_map/while/body/eval_jaxpr/cond
  323.5 14.0 %collective-permute-start = (bf16[208,2048]{1,0:T(8,128)(2,1)}, bf16[208,2048]{1,0:T(8,128)(2,1)S(1)}, u32[]{:S(2)}, u32[]{:S(2)}) collective-permute-start(bf16[208,2048]{1,0:T(8,128)(2,1)} %get-tuple-element.945), channel_id=1, source_target_pairs={{0,1},{1,2},{2,3},{4,5},{5,6},{6,7},{8,9},{9,10},{10,11},{12,13},{... | collective-permute-start | bytes 2555912 | tf_op jit(solution)/shard_map/while/body/eval_jaxpr/ppermute | solution.py:158
  327.7 8.3 %collective-permute-start.1 = (bf16[192,512]{1,0:T(8,128)(2,1)}, bf16[192,512]{1,0:T(8,128)(2,1)S(1)}, u32[]{:S(2)}, u32[]{:S(2)}) collective-permute-start(bf16[192,512]{1,0:T(8,128)(2,1)} %get-tuple-element.1026), channel_id=1, source_target_pairs={{0,4},{8,12},{1,5},{9,13},{2,6},{10,14},{3,7},{11,15},{16,20},{24,... | collective-permute-start | bytes 589832 | tf_op jit(solution)/shard_map/while/body/eval_jaxpr/ppermute | solution.py:159
  363.0 1.1 copy-start.3
  368.1 1.9 copy-start.4
  370.0 1.4 copy-start.1
  371.6 10.5 %copy-start = (bf16[400,256]{1,0:T(8,128)(2,1)S(1)}, bf16[400,256]{1,0:T(8,128)(2,1)}, u32[]{:S(2)}) copy-start(bf16[400,256]{1,0:T(8,128)(2,1)} %get-tuple-element.734) | copy-start | bytes 614404 | tf_op jit(solution)/shard_map/while/body/eval_jaxpr/cond
  432.0 13.0 %collective-permute-start = (bf16[208,2048]{1,0:T(8,128)(2,1)}, bf16[208,2048]{1,0:T(8,128)(2,1)S(1)}, u32[]{:S(2)}, u32[]{:S(2)}) collective-permute-start(bf16[208,2048]{1,0:T(8,128)(2,1)} %get-tuple-element.945), channel_id=1, source_target_pairs={{0,1},{1,2},{2,3},{4,5},{5,6},{6,7},{8,9},{9,10},{10,11},{12,13},{... | collective-permute-start | bytes 2555912 | tf_op jit(solution)/shard_map/while/body/eval_jaxpr/ppermute | solution.py:158
  436.0 7.3 collective-permute-start.1
  470.4 1.1 copy-start.3
  475.6 1.9 copy-start.4
  477.4 1.4 copy-start.1
  479.0 10.5 %copy-start = (bf16[400,256]{1,0:T(8,128)(2,1)S(1)}, bf16[400,256]{1,0:T(8,128)(2,1)}, u32[]{:S(2)}) copy-start(bf16[400,256]{1,0:T(8,128)(2,1)} %get-tuple-element.734) | copy-start | bytes 614404 | tf_op jit(solution)/shard_map/while/body/eval_jaxpr/cond
  539.4 14.0 %collective-permute-start = (bf16[208,2048]{1,0:T(8,128)(2,1)}, bf16[208,2048]{1,0:T(8,128)(2,1)S(1)}, u32[]{:S(2)}, u32[]{:S(2)}) collective-permute-start(bf16[208,2048]{1,0:T(8,128)(2,1)} %get-tuple-element.945), channel_id=1, source_target_pairs={{0,1},{1,2},{2,3},{4,5},{5,6},{6,7},{8,9},{9,10},{10,11},{12,13},{... | collective-permute-start | bytes 2555912 | tf_op jit(solution)/shard_map/while/body/eval_jaxpr/ppermute | solution.py:158
  544.5 7.3 collective-permute-start.1
  578.8 1.1 copy-start.3
  584.0 1.9 copy-start.4
  585.8 1.4 copy-start.1
  587.4 10.5 %copy-start = (bf16[400,256]{1,0:T(8,128)(2,1)S(1)}, bf16[400,256]{1,0:T(8,128)(2,1)}, u32[]{:S(2)}) copy-start(bf16[400,256]{1,0:T(8,128)(2,1)} %get-tuple-element.734) | copy-start | bytes 614404 | tf_op jit(solution)/shard_map/while/body/eval_jaxpr/cond
  647.8 13.9 %collective-permute-start = (bf16[208,2048]{1,0:T(8,128)(2,1)}, bf16[208,2048]{1,0:T(8,128)(2,1)S(1)}, u32[]{:S(2)}, u32[]{:S(2)}) collective-permute-start(bf16[208,2048]{1,0:T(8,128)(2,1)} %get-tuple-element.945), channel_id=1, source_target_pairs={{0,1},{1,2},{2,3},{4,5},{5,6},{6,7},{8,9},{9,10},{10,11},{12,13},{... | collective-permute-start | bytes 2555912 | tf_op jit(solution)/shard_map/while/body/eval_jaxpr/ppermute | solution.py:158
  652.6 7.4 collective-permute-start.1
Sparse Core Ops, SparseCore 0:
  680.6 57.0 all-gather.4

commit v2 on v1

v2 whole, which is shorter than its diff:
```python
import functools

import jax
import jax.numpy as jnp
import numpy as np
from jax import lax
from jax.experimental import pallas as pl
from jax.experimental.pallas import tpu as pltpu
from jax.sharding import PartitionSpec as P

EPS = 1e-5
THETA = 10000.0
TP_AXES = ('model', 'model2')
NEG = -1e30
BLK = 512
NBUF = 18
KEYS = 512
MESH_ID = pl.DeviceIdType.MESH

CHUNKS = (((4, 0), (1, 0), (5, 0), (3, 0)),
          ((0, 0), (1, 1), (2, 0), (3, 1)),
          ((0, 1), (4, 1), (2, 1), (5, 1)))


def rope_angles(positions, head_dim):
    half_dim = head_dim // 2
    inv_freq = jnp.power(THETA, jnp.arange(half_dim, dtype=jnp.float32) * (-2.0 / head_dim))
    angles = positions.astype(jnp.float32)[..., None] * inv_freq
    return jnp.cos(angles), jnp.sin(angles)


def dot32(a, b):
    return jnp.dot(a, b, preferred_element_type=jnp.float32)


def dot32t(a, b):
    return lax.dot_general(a, b, (((1,), (1,)), ((), ())), preferred_element_type=jnp.float32)


def norm_rows(x_f32, gain):
    inv_rms = lax.rsqrt(jnp.mean(x_f32 * x_f32, axis=-1, keepdims=True) + EPS)
    return (x_f32 * inv_rms * gain).astype(jnp.bfloat16)


def rope_block(v, cos_t, sin_t):
    lane = lax.broadcasted_iota(jnp.int32, (v.shape[0], 128), 1)
    first = (lane % 64) < 32
    out = []
    for c in range(v.shape[1] // 128):
        t = v[:, c * 128:(c + 1) * 128]
        other = jnp.where(first, pltpu.roll(t, 96, 1), pltpu.roll(t, 32, 1))
        out.append(t * cos_t + other * sin_t)
    return out


def mega_kernel(dims, x_mine, cos_ref, sin_ref, mask_ref, sel_ref, cosl_ref, sinl_ref, maskl_ref, ga_ref, gm_ref,
                w_qkv, w_out, w_gu, w_dt, kv_out, rows_out,
                wbuf, xin, ysend, kvst, nb, kst, vst, qbuf, obuf, hbuf, x1buf, yacc, hsel, x6, o6, rowbuf,
                wsem, act_send, act_recv, kv_send, kv_recv, kv_self, nb_send, nb_recv, row_send, row_recv, row_self):
    stages, width, num_k, rows, chunk, model_dim, q_cols, ff = dims
    n_dev = stages * width
    n_q = q_cols // BLK
    n_o = model_dim // BLK
    n_f = ff // BLK
    per = n_q + 1 + n_o + 3 * n_f
    stage = lax.axis_index('model')
    col = lax.axis_index('model2')
    me = stage * width + col
    last_stage = stages - 1
    f32 = jnp.float32
    bf16 = jnp.bfloat16

    def wslot(g):
        return lax.rem(g, NBUF)

    def fetch(g):
        b = lax.rem(g, per)
        slot = wslot(g)

        def go(src, j):
            pltpu.make_async_copy(src.at[:, pl.ds(pl.multiple_of(j * BLK, BLK), BLK)], wbuf.at[slot], wsem.at[slot]).start()

        @pl.when(b == 0)
        def _():
            go(w_qkv, n_q)

        @pl.when((b >= 1) & (b <= n_q))
        def _():
            go(w_qkv, b - 1)

        @pl.when((b > n_q) & (b <= n_q + n_o))
        def _():
            go(w_out, b - n_q - 1)

        f = b - (n_q + n_o + 1)

        @pl.when((f >= 0) & (lax.rem(f, 3) == 0))
        def _():
            go(w_gu, f // 3)

        @pl.when((f >= 0) & (lax.rem(f, 3) == 1))
        def _():
            go(w_gu, n_f + f // 3)

        @pl.when((f >= 0) & (lax.rem(f, 3) == 2))
        def _():
            go(w_dt, f // 3)

    def landed(g):
        slot = wslot(g)
        pltpu.make_async_copy(w_out.at[:, pl.ds(0, BLK)], wbuf.at[slot], wsem.at[slot]).wait()
        return slot

    def refill(g, total):
        @pl.when(g + NBUF < total)
        def _():
            fetch(g + NBUF)

    def first_fetch(g, carry):
        fetch(g)
        return carry
    lax.fori_loop(0, NBUF, first_fetch, 0)

    @pl.when(stage == 0)
    def _():
        for k in range(num_k):
            pltpu.make_async_copy(x_mine.at[k], xin.at[k], act_recv.at[k]).start()

    barrier = pltpu.get_barrier_semaphore()

    def peer(d):
        t = lax.rem(me + d, n_dev)
        return t // width, lax.rem(t, width)

    def greet(d, carry):
        c, z = peer(d)
        pl.semaphore_signal(barrier, inc=1, device_id={'model': c, 'model2': z}, device_id_type=MESH_ID)
        return carry
    lax.fori_loop(1, n_dev, greet, 0)

    kst[...] = jnp.zeros_like(kst)
    vst[...] = jnp.zeros_like(vst)

    def wait_x(k):
        @pl.when(stage == 0)
        def _():
            pltpu.make_async_copy(x_mine.at[k], xin.at[k], act_recv.at[k]).wait()

        @pl.when(stage > 0)
        def _():
            act_copy(k).wait_recv()

    def act_copy(k):
        return pltpu.make_async_remote_copy(src_ref=ysend.at[k], dst_ref=xin.at[k], send_sem=act_send.at[k], recv_sem=act_recv.at[k],
                                            device_id={'model': lax.rem(stage + 1, stages)}, device_id_type=MESH_ID)

    def kv_copy(k, d, src_dev):
        c, z = peer(d)
        return pltpu.make_async_remote_copy(src_ref=kvst.at[k, c], dst_ref=kv_out.at[src_dev // width, lax.rem(src_dev, width), k],
                                            send_sem=kv_send.at[k * n_dev + d], recv_sem=kv_recv.at[src_dev * num_k + k],
                                            device_id={'model': c, 'model2': z}, device_id_type=MESH_ID)

    def kv_local(k):
        return pltpu.make_async_copy(kvst.at[k, stage], kv_out.at[stage, col, k], kv_self.at[k])

    def nb_copy():
        return pltpu.make_async_remote_copy(src_ref=kvst.at[0], dst_ref=nb, send_sem=nb_send, recv_sem=nb_recv,
                                            device_id={'model2': lax.rem(col + 1, width)}, device_id_type=MESH_ID)

    def row_copy(d, src_col=None):
        c, z = peer(d)
        src = col if src_col is None else src_col
        return pltpu.make_async_remote_copy(src_ref=rowbuf, dst_ref=rows_out.at[src], send_sem=row_send.at[d], recv_sem=row_recv.at[src],
                                            device_id={'model': c, 'model2': z}, device_id_type=MESH_ID)

    lane_r = lax.broadcasted_iota(jnp.int32, (rows, 128), 1)
    low = lane_r < 64

    def stack(c, base, packed):
        n = packed.shape[0]
        lo = low[:n]
        turned = pltpu.roll(packed, 64, 1)
        zero = jnp.zeros_like(packed)
        kst[c, base:base + n, :] = jnp.where(lo, packed, zero).astype(bf16)
        kst[c, KEYS + base:KEYS + base + n, :] = jnp.where(lo, zero, turned).astype(bf16)
        vst[c, base:base + n, :] = jnp.where(lo, turned, zero).astype(bf16)
        vst[c, KEYS + base:KEYS + base + n, :] = jnp.where(lo, zero, packed).astype(bf16)

    def keys_values(k, slot):
        kv = dot32(hbuf[...], wbuf[slot])
        half = kv.shape[1] // 2
        keys = rope_block(kv[:, :half], cos_ref[k], sin_ref[k])
        for c in range(stages):
            kt = keys[c // 2]
            vt = kv[:, half + (c // 2) * 128:half + (c // 2 + 1) * 128]
            if c % 2 == 0:
                packed = jnp.where(low, kt, pltpu.roll(vt, 64, 1))
            else:
                packed = jnp.where(low, pltpu.roll(kt, 64, 1), vt)
            packed = packed.astype(bf16)
            kvst[k, c] = packed
            stack(c, chunk, packed.astype(f32))

        @pl.when(k == 0)
        def _():
            pl.semaphore_wait(barrier, n_dev - 1)

            @pl.when(lax.rem(col, 2) == 0)
            def _():
                nb_copy().start()

        def send(d, carry):
            kv_copy(k, d, me).start()
            return carry
        lax.fori_loop(1, n_dev, send, 0)
        kv_local(k).start()

        use_nb = (k == num_k - 1) & (lax.rem(col, 2) == 1)

        @pl.when(use_nb)
        def _():
            nb_copy().wait_recv()
            for c in range(stages):
                stack(c, 0, nb[c, :chunk].astype(f32))

        @pl.when((k > 0) & jnp.logical_not(use_nb))
        def _():
            for c in range(stages):
                stack(c, 0, kvst[lax.max(k - 1, 0), c, :chunk].astype(f32))

    def attend(q_ref, o_ref, m_ref, n_rows):
        pairs = q_cols // 128
        per_c = pairs // stages

        def pair(i, carry):
            c = i // per_c
            at = pl.ds(pl.multiple_of(i * 128, 128), 128)
            s = dot32t(q_ref[:, at], kst[c])
            parts = []
            for e in range(2):
                se = jnp.where(m_ref[...] > 0.5, s[:, e * KEYS:(e + 1) * KEYS], NEG)
                ex = jnp.exp(se - jnp.max(se, axis=-1, keepdims=True))
                inv = 1.0 / jnp.sum(ex, axis=-1, keepdims=True)
                parts.append((ex * inv).astype(bf16))
            o_ref[:, at] = dot32(jnp.concatenate(parts, axis=1), vst[c]).astype(bf16)
            return carry
        lax.fori_loop(0, pairs, pair, 0)

    scale = 64 ** -0.5

    def block_at(j):
        return pl.ds(pl.multiple_of(j * BLK, BLK), BLK)

    def act_of(h, slot_g, slot_u):
        g = dot32(h, wbuf[slot_g])
        u = dot32(h, wbuf[slot_u])
        return (g * jax.nn.sigmoid(g) * u).astype(bf16)

    @pl.when(stage < last_stage)
    def _():
        total = per * num_k

        def one_chunk(k, carry):
            g0 = k * per
            wait_x(k)
            hbuf[...] = norm_rows(xin[k].astype(f32), ga_ref[...])
            keys_values(k, landed(g0))
            refill(g0, total)

            def q_block(j, cc):
                g = g0 + 1 + j
                slot = landed(g)
                v = rope_block(dot32(hbuf[...], wbuf[slot]), cos_ref[k], sin_ref[k])
                for i in range(BLK // 128):
                    qbuf[:, pl.ds(pl.multiple_of(j * BLK + i * 128, 128), 128)] = (v[i] * scale).astype(bf16)
                refill(g, total)
                return cc
            lax.fori_loop(0, n_q, q_block, 0)

            attend(qbuf, obuf, mask_ref.at[k], rows)

            def o_block(j, cc):
                g = g0 + 1 + n_q + j
                slot = landed(g)
                x1buf[:, block_at(j)] = (xin[k, :, block_at(j)].astype(f32) + dot32(obuf[...], wbuf[slot])).astype(bf16)
                refill(g, total)
                return cc
            lax.fori_loop(0, n_o, o_block, 0)

            x1 = x1buf[...].astype(f32)
            hbuf[...] = norm_rows(x1, gm_ref[...])
            yacc[...] = jnp.zeros_like(yacc)

            def f_block(j, cc):
                g = g0 + 1 + n_q + n_o + 3 * j
                sg = landed(g)
                su = landed(g + 1)
                a = act_of(hbuf[...], sg, su)
                refill(g, total)
                refill(g + 1, total)
                sd = landed(g + 2)
                yacc[...] += dot32t(a, wbuf[sd])
                refill(g + 2, total)
                return cc
            lax.fori_loop(0, n_f, f_block, 0)
            ysend[k] = (x1buf[...].astype(f32) + yacc[...]).astype(bf16)
            act_copy(k).start()
            return carry
        lax.fori_loop(0, num_k, one_chunk, 0)

    @pl.when(stage == last_stage)
    def _():
        small = x6.shape[0]
        x6[...] = jnp.zeros_like(x6)
        o6[...] = jnp.zeros_like(o6)
        row_id = lax.broadcasted_iota(jnp.int32, (small, q_cols), 0)
        for b in range(n_q + 1):
            landed(b)

        def one_chunk(k, carry):
            wait_x(k)
            hbuf[...] = norm_rows(xin[k].astype(f32), ga_ref[...])
            keys_values(k, 0)
            sel = sel_ref[k]
            x6[...] += dot32(sel, xin[k])
            hsel[...] = dot32(sel, hbuf[...]).astype(bf16)

            def q_block(j, cc):
                v = rope_block(dot32(hsel[...], wbuf[1 + j]), cosl_ref[k], sinl_ref[k])
                for i in range(BLK // 128):
                    qbuf[:small, pl.ds(pl.multiple_of(j * BLK + i * 128, 128), 128)] = (v[i] * scale).astype(bf16)
                return cc
            lax.fori_loop(0, n_q, q_block, 0)
            attend(qbuf.at[:small], obuf.at[:small], maskl_ref.at[k], small)
            o6[...] = jnp.where(row_id // 2 == k, obuf[:small].astype(f32), o6[...])
            return carry
        lax.fori_loop(0, num_k, one_chunk, 0)
        for b in range(n_q + 1):
            refill(b, per)
        o_in = o6[...].astype(bf16)

        def o_block(j, cc):
            g = 1 + n_q + j
            slot = landed(g)
            x1buf[:small, block_at(j)] = (x6[:, block_at(j)] + dot32(o_in, wbuf[slot])).astype(bf16)
            refill(g, per)
            return cc
        lax.fori_loop(0, n_o, o_block, 0)
        x1 = x1buf[:small].astype(f32)
        hsel[...] = norm_rows(x1, gm_ref[...])
        yacc[:small] = jnp.zeros_like(x1)

        def f_block(j, cc):
            g = 1 + n_q + n_o + 3 * j
            sg = landed(g)
            su = landed(g + 1)
            a = act_of(hsel[...], sg, su)
            refill(g, per)
            refill(g + 1, per)
            sd = landed(g + 2)
            yacc[:small] += dot32t(a, wbuf[sd])
            refill(g + 2, per)
            return cc
        lax.fori_loop(0, n_f, f_block, 0)
        rowbuf[...] = (x1buf[:small].astype(f32) + yacc[:small]).astype(bf16)

        def send(d, carry):
            row_copy(d).start()
            return carry
        lax.fori_loop(1, n_dev, send, 0)
        pltpu.make_async_copy(rowbuf, rows_out.at[col], row_self).start()

    def drain(d, carry):
        src = lax.rem(me + d, n_dev)
        for k in range(num_k):
            kv_copy(k, d, me).wait_send()
            kv_copy(k, d, src).wait_recv()
        return carry
    lax.fori_loop(1, n_dev, drain, 0)
    for k in range(num_k):
        kv_local(k).wait()

    @pl.when(lax.rem(col, 2) == 0)
    def _():
        nb_copy().wait_send()

    @pl.when(stage < last_stage)
    def _():
        for k in range(num_k):
            act_copy(k).wait_send()

    @pl.when(stage == last_stage)
    def _():
        def sent(d, carry):
            row_copy(d).wait_send()
            return carry
        lax.fori_loop(1, n_dev, sent, 0)
        pltpu.make_async_copy(rowbuf, rows_out.at[col], row_self).wait()

    for z in range(width):
        @pl.when((stage < last_stage) | (col != z))
        def _():
            row_copy(1, z).wait_recv()


def solution(mesh):
    stages = mesh.shape['model']
    width = mesh.shape['model2']
    stage_spec = P('model', None, None)
    in_specs = (P('replica', None, None, None), P('replica', None), P('replica', None),
                stage_spec, stage_spec, stage_spec, stage_spec, P(None, None), P(None, None),
                P(None, None, TP_AXES, None), P(None, None, TP_AXES, None), P(None, None, TP_AXES, None),
                P(None, TP_AXES, None, None), P(None, None, TP_AXES), P(None, None, TP_AXES), P(None, TP_AXES, None))
    cache_spec = P(None, 'replica', None, TP_AXES, None)
    out_specs = (P('replica', None), P('replica', None), cache_spec, cache_spec)
    num_k = len(CHUNKS)
    pid_tab = np.array([[c[0] for c in row] for row in CHUNKS], np.int32)
    half_tab = np.array([[c[1] for c in row] for row in CHUNKS], np.int32)

    def shard_body(x_prompt, lengths, x_new, st_qkv, st_out, st_gateup, st_down_t, gain_attn, gain_mlp, tp_query, tp_key, tp_value, tp_out, tp_gate, tp_up, tp_down):
        seq_len, model_dim = x_prompt.shape[2:]
        batch = x_new.shape[0]
        head_dim = tp_query.shape[-1]
        w_qkv, w_out, w_gateup, w_down_t = st_qkv[0], st_out[0], st_gateup[0], st_down_t[0]
        q_cols = w_out.shape[0]
        ff = w_down_t.shape[1]
        chunk = seq_len // 2
        rows = chunk + 16
        small = 16
        stage = lax.axis_index('model')
        col = lax.axis_index('model2')
        g_attn = lax.dynamic_slice_in_dim(gain_attn, stage, 1, 0)
        g_mlp = lax.dynamic_slice_in_dim(gain_mlp, stage, 1, 0)
        lens = lengths.reshape(batch)
        x_chunks = x_prompt.reshape(batch, 2, chunk, model_dim)
        pids = jnp.asarray(pid_tab)[:, col]
        halves = jnp.asarray(half_tab)[:, col]
        x_mine = jnp.stack([jnp.concatenate([x_chunks[pids[k], halves[k]], x_new[pids[k]][None], jnp.zeros((rows - chunk - 1, model_dim), jnp.bfloat16)], axis=0)
                            for k in range(num_k)])
        len_k = lens[pids][:, None]
        half_k = halves[:, None]
        row_i = jnp.arange(rows)[None]
        pos = jnp.where(row_i < chunk, half_k * chunk + row_i, len_k)

        def tables(p):
            cos_h, sin_h = rope_angles(p, head_dim)
            return jnp.concatenate([cos_h] * 4, axis=-1), jnp.concatenate([-sin_h, sin_h] * 2, axis=-1)

        def masks(p, dec):
            j = jnp.arange(KEYS)[None, None]
            kpos = jnp.where(j < chunk, j, half_k[..., None] * chunk + j - chunk)
            seen = jnp.where(j < chunk, half_k[..., None] == 1, j < 2 * chunk)
            m = seen & (kpos < len_k[..., None]) & (dec | (kpos <= p[..., None]))
            return (m | (dec & (j == 2 * chunk))).astype(jnp.float32)

        cos_t, sin_t = tables(pos)
        mask = masks(pos, jnp.broadcast_to(row_i >= chunk, pos.shape)[..., None])
        s_i = jnp.arange(small)[None]
        is_dec = jnp.broadcast_to(s_i % 2 == 1, (num_k, small))
        last_i = jnp.clip(len_k - 1 - half_k * chunk, 0, chunk - 1)
        pick = jnp.where(is_dec, chunk, last_i)
        mine = s_i // 2 == jnp.arange(num_k)[:, None]
        sel = (mine[..., None] & (pick[..., None] == row_i[:, None])).astype(jnp.bfloat16)
        pos_l = jnp.where(is_dec, len_k, half_k * chunk + last_i)
        cos_l, sin_l = tables(pos_l)
        mask_l = masks(pos_l, is_dec[..., None])

        dims = (stages, width, num_k, rows, chunk, model_dim, q_cols, ff)
        bf16, f32 = jnp.bfloat16, jnp.float32
        n_dev = stages * width
        vm = pl.BlockSpec(memory_space=pltpu.VMEM)
        hbm = pl.BlockSpec(memory_space=pl.ANY)
        dma = pltpu.SemaphoreType.DMA
        kv_all, rows_all = pl.pallas_call(
            functools.partial(mega_kernel, dims),
            out_shape=(jax.ShapeDtypeStruct((stages, width, num_k, rows, 128), bf16),
                       jax.ShapeDtypeStruct((width, small, model_dim), bf16)),
            in_specs=[hbm] + [vm] * 9 + [hbm] * 4,
            out_specs=(hbm, hbm),
            scratch_shapes=[
                pltpu.VMEM((NBUF, model_dim, BLK), bf16),
                pltpu.VMEM((num_k, rows, model_dim), bf16),
                pltpu.VMEM((num_k, rows, model_dim), bf16),
                pltpu.VMEM((num_k, stages, rows, 128), bf16),
                pltpu.VMEM((stages, rows, 128), bf16),
                pltpu.VMEM((stages, 2 * KEYS, 128), bf16),
                pltpu.VMEM((stages, 2 * KEYS, 128), bf16),
                pltpu.VMEM((rows, q_cols), bf16),
                pltpu.VMEM((rows, q_cols), bf16),
                pltpu.VMEM((rows, model_dim), bf16),
                pltpu.VMEM((rows, model_dim), bf16),
                pltpu.VMEM((rows, model_dim), f32),
                pltpu.VMEM((small, model_dim), bf16),
                pltpu.VMEM((small, model_dim), f32),
                pltpu.VMEM((small, q_cols), f32),
                pltpu.VMEM((small, model_dim), bf16),
                dma((NBUF,)), dma((num_k,)), dma((num_k,)), dma((num_k * n_dev,)), dma((num_k * n_dev,)), dma((num_k,)),
                dma, dma, dma((n_dev,)), dma((width,)), dma,
            ],
            compiler_params=pltpu.CompilerParams(collective_id=0, has_side_effects=True, vmem_limit_bytes=67043328),
            name='pipeline',
        )(x_mine, cos_t, sin_t, mask, sel, cos_l, sin_l, mask_l, g_attn, g_mlp, w_qkv, w_out, w_gateup, w_down_t)

        where_a = {}
        where_b = {}
        for k in range(num_k):
            for z in range(width):
                (where_b if CHUNKS[k][z][1] else where_a)[CHUNKS[k][z][0]] = (z, k)
        dec = jnp.stack([rows_all[where_b[p][0], 2 * where_b[p][1] + 1] for p in range(batch)])
        last = jnp.stack([jnp.where(lens[p] > chunk, rows_all[where_b[p][0], 2 * where_b[p][1]], rows_all[where_a[p][0], 2 * where_a[p][1]])
                          for p in range(batch)])
        full_kv = jnp.stack([jnp.concatenate([kv_all[:, where_a[p][0], where_a[p][1], :chunk],
                                              kv_all[:, where_b[p][0], where_b[p][1], :chunk + 1]], axis=1)
                             for p in range(batch)], axis=1)
        k_full = full_kv[:, :, :, None, :head_dim]
        v_full = full_kv[:, :, :, None, head_dim:]
        return dec, last, k_full, v_full

    return jax.shard_map(shard_body, mesh=mesh, in_specs=in_specs, out_specs=out_specs, check_vma=False)
```

time: 785 us -> 334 us (0.43)
  the two profiles are of different devices: /device:TPU:0 before, /device:TPU:5 now
where the time goes in v2:
time: 334 us; the launch traced here: 333 us
  Pallas kernels  282 us (84%)
  local copies, waits for them, and re-layouts  22.1 us (7%)
  between operations  16.3 us (5%)
  other arithmetic  12.7 us (4%)
    pallas_call x1, Pallas kernels, shard_body(): pl.pallas_call(functools.partial(mega_kernel, dims), out_shape=(jax.Shape...  282 us

profile of v2, /device:TPU:5, one launch (start us, length us, event | category | flops | bytes accessed | tf_op | source)
XLA Modules:
  0.0 332.8 jit_solution(13602310889555055003)
XLA Ops:
  0.6 0.8 reshape.631
  1.4 0.7 compare_bitcast_fusion
  2.1 0.1 pad.39.clone
  2.2 0.7 fusion.17
  2.9 0.6 fusion.25
  9.3 0.6 fusion.23
  13.8 0.6 gather_fusion
  14.5 0.7 add_bitcast_fusion
  15.2 0.1 compare_and_fusion
  15.2 0.6 fusion.24
  21.7 0.1 broadcast_select_fusion.6
  21.7 0.1 add_select_fusion.1
  21.8 0.1 add_select_fusion
  21.9 1.4 constant_dynamic-slice_fusion
  23.3 0.7 fusion.8.sel_ref
  24.0 0.9 constant_dynamic-slice_fusion.4
  24.9 0.2 fusion.15
  25.0 0.7 pad_maximum_fusion.3
  25.8 0.7 or_convert_fusion.1.maskl_ref
  26.5 1.2 fusion.6
  27.7 1.4 pad_maximum_fusion.1
  29.1 1.4 or_convert_fusion.mask_ref
  30.5 1.8 dynamic-slice_bitcast_fusion.2
  32.2 0.8 maximum_bitcast_fusion
  33.0 1.8 pad_maximum_fusion.x_mine
  34.8 281.7 %pipeline.1 = (bf16[4,4,3,208,128]{4,3,2,1,0:T(8,128)(2,1)}, bf16[4,16,2048]{2,1,0:T(8,128)(2,1)}) custom-call(bf16[3,208,2048]{2,1,0:T(8,128)(2,1)} %pad_maximum_fusion.x_mine, f32[3,208,128]{2,1,0:T(8,128)} %get-tuple-element.79.cos_ref, f32[3,208,128]{2,1,0:T(8,128)} %get-tuple-element.80.sin_ref, f32[3,208,512]{2,1,0:T(8,128)} %or_convert_fusion.mask_ref, ...), custom_call_target="tpu_custom_call" | custom-call | tf_op jit(solution)/shard_map/pipeline/pallas_call | solution.py:474
  316.5 0.9 slice_bitcast_fusion.15
  317.3 1.1 fusion.14
  318.5 0.7 stack.50
  319.2 0.7 stack.49
  319.9 0.9 slice_bitcast_fusion.7
  320.8 1.4 slice_bitcast_fusion.2
  322.2 1.4 slice_bitcast_fusion.8
  323.7 0.1 fusion.1
  323.8 0.1 fusion.2
  323.8 0.1 fusion.3
  323.9 0.1 fusion.4
  324.0 0.1 fusion.5
  324.0 2.3 slice_bitcast_fusion
  326.3 4.1 %copy.40 = bf16[4,6,385,1,64]{2,4,3,1,0:T(8,128)(2,1)} copy(bf16[4,6,385,1,64]{4,2,0,1,3:T(8,128)(2,1)} %get-tuple-element.30) | data formatting | bytes 2365440
  330.4 2.4 copy.39
  (11 shorter events, 0.1 us)

commit v3 on v2

--- a/solution.py
+++ b/solution.py
@@ -20,13 +20,6 @@
 CHUNKS = (((4, 0), (1, 0), (5, 0), (3, 0)),
           ((0, 0), (1, 1), (2, 0), (3, 1)),
           ((0, 1), (4, 1), (2, 1), (5, 1)))
-
-
-def rope_angles(positions, head_dim):
-    half_dim = head_dim // 2
-    inv_freq = jnp.power(THETA, jnp.arange(half_dim, dtype=jnp.float32) * (-2.0 / head_dim))
-    angles = positions.astype(jnp.float32)[..., None] * inv_freq
-    return jnp.cos(angles), jnp.sin(angles)
 
 
 def dot32(a, b):
@@ -53,10 +46,12 @@
     return out
 
 
-def mega_kernel(dims, x_mine, cos_ref, sin_ref, mask_ref, sel_ref, cosl_ref, sinl_ref, maskl_ref, ga_ref, gm_ref,
-                w_qkv, w_out, w_gu, w_dt, kv_out, rows_out,
-                wbuf, xin, ysend, kvst, nb, kst, vst, qbuf, obuf, hbuf, x1buf, yacc, hsel, x6, o6, rowbuf,
-                wsem, act_send, act_recv, kv_send, kv_recv, kv_self, nb_send, nb_recv, row_send, row_recv, row_self):
+def mega_kernel(dims, lens, x_prompt, x_new, tab_cos, tab_sin, ga_all, gm_all,
+                w_qkv, w_out, w_gu, w_dt, kv_out, dec_out, last_out,
+                wbuf, xin, ysend, kvst, nb, kst, vst, qbuf, obuf, hbuf, x1buf, yacc, cosb, sinb, maskb, coslb, sinlb, masklb,
+                hsel, x6, o6, hg, yparts, yrecv, rowbuf, rland,
+                wsem, act_send, act_recv, kv_send, kv_recv, kv_self, nb_send, nb_recv, row_send, row_recv,
+                h_send, h_recv, p_send, p_recv):
     stages, width, num_k, rows, chunk, model_dim, q_cols, ff = dims
     n_dev = stages * width
     n_q = q_cols // BLK
@@ -69,6 +64,54 @@
     last_stage = stages - 1
     f32 = jnp.float32
     bf16 = jnp.bfloat16
+    small = x6.shape[0]
+    row_count = x_prompt.shape[1]
+    ga_ref = ga_all.at[pl.ds(stage, 1)]
+    gm_ref = gm_all.at[pl.ds(stage, 1)]
+
+    def here(k, table):
+        out = table[0][0]
+        for kk in range(num_k):
+            for z in range(width):
+                out = jnp.where((k == kk) & (col == z), table[kk][z], out)
+        return out
+
+    len_tab = [[lens[p // row_count, p % row_count] for p, _ in line] for line in CHUNKS]
+    half_tab = [[h for _, h in line] for line in CHUNKS]
+
+    def iota(shape, dim):
+        return lax.broadcasted_iota(jnp.int32, shape, dim)
+
+    def visible(j, pos, dec, length, half):
+        kpos = jnp.where(j < chunk, j, half * chunk + j - chunk)
+        seen = (j >= chunk * (1 - half)) & (j < 2 * chunk) & (kpos < length) & (dec | (kpos <= pos))
+        return jnp.where(seen | (dec & (j == 2 * chunk)), 1.0, 0.0)
+
+    def set_tables(k):
+        length, half = here(k, len_tab), here(k, half_tab)
+        at = pl.ds(pl.multiple_of(half * chunk, 8), chunk)
+        t_i = iota(tab_cos.shape, 0)
+        odd = iota((small, 128), 0) % 2 == 1
+        for tab, buf, buf_l in ((tab_cos, cosb, coslb), (tab_sin, sinb, sinlb)):
+            buf[:chunk] = tab[at, :]
+            at_len = jnp.sum(jnp.where(t_i == length, tab[...], 0.0), axis=0, keepdims=True)
+            buf[chunk:] = jnp.broadcast_to(at_len, (rows - chunk, 128))
+
+            @pl.when(stage == last_stage)
+            def _():
+                at_last = jnp.sum(jnp.where(t_i == length - 1, tab[...], 0.0), axis=0, keepdims=True)
+                buf_l[...] = jnp.where(odd, at_len, at_last)
+
+        @pl.when(stage < last_stage)
+        def _():
+            i = iota((rows, KEYS), 0)
+            dec = i >= chunk
+            maskb[...] = visible(iota((rows, KEYS), 1), jnp.where(dec, length, half * chunk + i), dec, length, half)
+
+        @pl.when(stage == last_stage)
+        def _():
+            dec = iota((small, KEYS), 0) % 2 == 1
+            masklb[...] = visible(iota((small, KEYS), 1), jnp.where(dec, length, length - 1), dec, length, half)
 
     def wslot(g):
         return lax.rem(g, NBUF)
@@ -105,6 +148,25 @@
         @pl.when((f >= 0) & (lax.rem(f, 3) == 2))
         def _():
             go(w_dt, f // 3)
+
+    def fetch_last(b):
+        def go(src, j):
+            pltpu.make_async_copy(src.at[:, pl.ds(pl.multiple_of(j * BLK, BLK), BLK)], wbuf.at[b], wsem.at[b]).start()
+        if b == 0:
+            go(w_qkv, n_q)
+        elif b <= n_q:
+            go(w_qkv, b - 1)
+        elif b <= n_q + n_o:
+            go(w_out, b - n_q - 1)
+        else:
+            i = b - (n_q + n_o + 1)
+            j = lax.min(col + (i // 3) * width, n_f - 1)
+            if i % 3 == 0:
+                go(w_gu, j)
+            elif i % 3 == 1:
+                go(w_gu, n_f + j)
+            else:
+                go(w_dt, j)
 
     def landed(g):
         slot = wslot(g)
@@ -119,12 +181,29 @@
     def first_fetch(g, carry):
         fetch(g)
         return carry
-    lax.fori_loop(0, NBUF, first_fetch, 0)
+    n_mine = (n_f + width - 1) // width
+    n_last = n_q + 1 + n_o + 3 * n_mine
+
+    def x_copy(k, z):
+        p, h = CHUNKS[k][z]
+        return pltpu.make_async_copy(x_prompt.at[p // row_count, p % row_count, pl.ds(h * chunk, chunk)], xin.at[k, pl.ds(0, chunk)], act_recv.at[k])
 
     @pl.when(stage == 0)
     def _():
-        for k in range(num_k):
-            pltpu.make_async_copy(x_mine.at[k], xin.at[k], act_recv.at[k]).start()
+        for z in range(width):
+            @pl.when(col == z)
+            def _():
+                for k in range(num_k):
+                    x_copy(k, z).start()
+
+    @pl.when(stage < last_stage)
+    def _():
+        lax.fori_loop(0, NBUF, first_fetch, 0)
+
+    @pl.when(stage == last_stage)
+    def _():
+        for b in range(n_last):
+            fetch_last(b)
 
     barrier = pltpu.get_barrier_semaphore()
 
@@ -138,13 +217,23 @@
         return carry
     lax.fori_loop(1, n_dev, greet, 0)
 
+    @pl.when(stage == 0)
+    def _():
+        for z in range(width):
+            @pl.when(col == z)
+            def _():
+                for k in range(num_k):
+                    p = CHUNKS[k][z][0]
+                    new_row = jnp.broadcast_to(x_new[p:p + 1, :].astype(f32), (rows - chunk, model_dim))
+                    xin[k, chunk:] = jnp.where(iota(new_row.shape, 0) == 0, new_row, 0.0).astype(bf16)
+
     kst[...] = jnp.zeros_like(kst)
     vst[...] = jnp.zeros_like(vst)
 
     def wait_x(k):
         @pl.when(stage == 0)
         def _():
-            pltpu.make_async_copy(x_mine.at[k], xin.at[k], act_recv.at[k]).wait()
+            pltpu.make_async_copy(x_prompt.at[0, 0, pl.ds(0, chunk)], xin.at[k, pl.ds(0, chunk)], act_recv.at[k]).wait()
 
         @pl.when(stage > 0)
         def _():
@@ -167,11 +256,19 @@
         return pltpu.make_async_remote_copy(src_ref=kvst.at[0], dst_ref=nb, send_sem=nb_send, recv_sem=nb_recv,
                                             device_id={'model2': lax.rem(col + 1, width)}, device_id_type=MESH_ID)
 
-    def row_copy(d, src_col=None):
+    def row_copy(d, src_col):
         c, z = peer(d)
-        src = col if src_col is None else src_col
-        return pltpu.make_async_remote_copy(src_ref=rowbuf, dst_ref=rows_out.at[src], send_sem=row_send.at[d], recv_sem=row_recv.at[src],
+        return pltpu.make_async_remote_copy(src_ref=rowbuf, dst_ref=rland.at[src_col], send_sem=row_send.at[d], recv_sem=row_recv.at[src_col],
                                             device_id={'model': c, 'model2': z}, device_id_type=MESH_ID)
+
+    def h_copy(d, src_col):
+        return pltpu.make_async_remote_copy(src_ref=hsel, dst_ref=hg.at[src_col], send_sem=h_send.at[d], recv_sem=h_recv.at[src_col],
+                                            device_id={'model2': lax.rem(col + d, width)}, device_id_type=MESH_ID)
+
+    def p_copy(d, src_col):
+        z = lax.rem(col + d, width)
+        return pltpu.make_async_remote_copy(src_ref=yparts.at[z], dst_ref=yrecv.at[src_col], send_sem=p_send.at[d], recv_sem=p_recv.at[src_col],
+                                            device_id={'model2': z}, device_id_type=MESH_ID)
 
     lane_r = lax.broadcasted_iota(jnp.int32, (rows, 128), 1)
     low = lane_r < 64
@@ -189,7 +286,7 @@
     def keys_values(k, slot):
         kv = dot32(hbuf[...], wbuf[slot])
         half = kv.shape[1] // 2
-        keys = rope_block(kv[:, :half], cos_ref[k], sin_ref[k])
+        keys = rope_block(kv[:, :half], cosb[...], sinb[...])
         for c in range(stages):
             kt = keys[c // 2]
             vt = kv[:, half + (c // 2) * 128:half + (c // 2 + 1) * 128]
@@ -209,10 +306,6 @@
             def _():
                 nb_copy().start()
 
-        def send(d, carry):
-            kv_copy(k, d, me).start()
-            return carry
-        lax.fori_loop(1, n_dev, send, 0)
         kv_local(k).start()
 
         use_nb = (k == num_k - 1) & (lax.rem(col, 2) == 1)
@@ -262,6 +355,7 @@
 
         def one_chunk(k, carry):
             g0 = k * per
+            set_tables(k)
             wait_x(k)
             hbuf[...] = norm_rows(xin[k].astype(f32), ga_ref[...])
             keys_values(k, landed(g0))
@@ -270,18 +364,19 @@
             def q_block(j, cc):
                 g = g0 + 1 + j
                 slot = landed(g)
-                v = rope_block(dot32(hbuf[...], wbuf[slot]), cos_ref[k], sin_ref[k])
+                v = rope_block(dot32(hbuf[...], wbuf[slot]), cosb[...], sinb[...])
                 for i in range(BLK // 128):
                     qbuf[:, pl.ds(pl.multiple_of(j * BLK + i * 128, 128), 128)] = (v[i] * scale).astype(bf16)
                 refill(g, total)
                 return cc
             lax.fori_loop(0, n_q, q_block, 0)
 
-            attend(qbuf, obuf, mask_ref.at[k], rows)
+            attend(qbuf, obuf, maskb, rows)
 
             def o_block(j, cc):
                 g = g0 + 1 + n_q + j
                 slot = landed(g)
+                kv_copy(k, 1 + j, me).start()
                 x1buf[:, block_at(j)] = (xin[k, :, block_at(j)].astype(f32) + dot32(obuf[...], wbuf[slot])).astype(bf16)
                 refill(g, total)
                 return cc
@@ -295,6 +390,7 @@
                 g = g0 + 1 + n_q + n_o + 3 * j
                 sg = landed(g)
                 su = landed(g + 1)
+                kv_copy(k, 1 + n_o + j, me).start()
                 a = act_of(hbuf[...], sg, su)
                 refill(g, total)
                 refill(g + 1, total)
@@ -310,65 +406,79 @@
 
     @pl.when(stage == last_stage)
     def _():
-        small = x6.shape[0]
         x6[...] = jnp.zeros_like(x6)
         o6[...] = jnp.zeros_like(o6)
-        row_id = lax.broadcasted_iota(jnp.int32, (small, q_cols), 0)
+        row_id = iota((small, q_cols), 0)
         for b in range(n_q + 1):
             landed(b)
 
         def one_chunk(k, carry):
+            set_tables(k)
             wait_x(k)
             hbuf[...] = norm_rows(xin[k].astype(f32), ga_ref[...])
             keys_values(k, 0)
-            sel = sel_ref[k]
+
+            def send(d, cc):
+                kv_copy(k, d, me).start()
+                return cc
+            lax.fori_loop(1, n_dev, send, 0)
+            r = iota((small, rows), 0)
+            last_i = lax.clamp(0, here(k, len_tab) - 1 - here(k, half_tab) * chunk, chunk - 1)
+            pick = jnp.where(r % 2 == 1, chunk, last_i)
+            sel = jnp.where((r // 2 == k) & (iota((small, rows), 1) == pick), 1.0, 0.0).astype(bf16)
             x6[...] += dot32(sel, xin[k])
-            hsel[...] = dot32(sel, hbuf[...]).astype(bf16)
+            hs = dot32(sel, hbuf[...]).astype(bf16)
 
             def q_block(j, cc):
-                v = rope_block(dot32(hsel[...], wbuf[1 + j]), cosl_ref[k], sinl_ref[k])
+                v = rope_block(dot32(hs, wbuf[1 + j]), coslb[...], sinlb[...])
                 for i in range(BLK // 128):
                     qbuf[:small, pl.ds(pl.multiple_of(j * BLK + i * 128, 128), 128)] = (v[i] * scale).astype(bf16)
                 return cc
             lax.fori_loop(0, n_q, q_block, 0)
-            attend(qbuf.at[:small], obuf.at[:small], maskl_ref.at[k], small)
+            attend(qbuf.at[:small], obuf.at[:small], masklb, small)
             o6[...] = jnp.where(row_id // 2 == k, obuf[:small].astype(f32), o6[...])
             return carry
         lax.fori_loop(0, num_k, one_chunk, 0)
-        for b in range(n_q + 1):
-            refill(b, per)
+        for b in range(n_q + 1, n_last):
+            landed(b)
         o_in = o6[...].astype(bf16)
 
         def o_block(j, cc):
-            g = 1 + n_q + j
-            slot = landed(g)
-            x1buf[:small, block_at(j)] = (x6[:, block_at(j)] + dot32(o_in, wbuf[slot])).astype(bf16)
-            refill(g, per)
+            x1buf[:small, block_at(j)] = (x6[:, block_at(j)] + dot32(o_in, wbuf[1 + n_q + j])).astype(bf16)
             return cc
         lax.fori_loop(0, n_o, o_block, 0)
         x1 = x1buf[:small].astype(f32)
         hsel[...] = norm_rows(x1, gm_ref[...])
-        yacc[:small] = jnp.zeros_like(x1)
-
-        def f_block(j, cc):
-            g = 1 + n_q + n_o + 3 * j
-            sg = landed(g)
-            su = landed(g + 1)
-            a = act_of(hsel[...], sg, su)
-            refill(g, per)
-            refill(g + 1, per)
-            sd = landed(g + 2)
-            yacc[:small] += dot32t(a, wbuf[sd])
-            refill(g + 2, per)
+        for d in range(1, width):
+            h_copy(d, col).start()
+        hg[col] = hsel[...]
+        for d in range(1, width):
+            h_copy(d, lax.rem(col + d, width)).wait_recv()
+        h_all = jnp.concatenate([hg[z].astype(f32) for z in range(width)], axis=0).astype(bf16)
+        yacc[:width * small] = jnp.zeros((width * small, model_dim), f32)
+
+        def f_block(i, cc):
+            b = 1 + n_q + n_o + 3 * i
+
+            @pl.when(col + width * i < n_f)
+            def _():
+                yacc[:width * small] += dot32t(act_of(h_all, b, b + 1), wbuf[b + 2])
             return cc
-        lax.fori_loop(0, n_f, f_block, 0)
-        rowbuf[...] = (x1buf[:small].astype(f32) + yacc[:small]).astype(bf16)
+        lax.fori_loop(0, n_mine, f_block, 0)
+        for z in range(width):
+            yparts[z] = yacc[z * small:(z + 1) * small]
+        for d in range(1, width):
+            p_copy(d, col).start()
+        yrecv[col] = yparts[col]
+        for d in range(1, width):
+            p_copy(d, lax.rem(col + d, width)).wait_recv()
+        rowbuf[...] = (x1 + (yrecv[0] + yrecv[1] + yrecv[2] + yrecv[3])).astype(bf16)
 
         def send(d, carry):
-            row_copy(d).start()
+            row_copy(d, col).start()
             return carry
         lax.fori_loop(1, n_dev, send, 0)
-        pltpu.make_async_copy(rowbuf, rows_out.at[col], row_self).start()
+        rland[col] = rowbuf[...]
 
     def drain(d, carry):
         src = lax.rem(me + d, n_dev)
@@ -391,16 +501,32 @@
 
     @pl.when(stage == last_stage)
     def _():
+        for d in range(1, width):
+            h_copy(d, col).wait_send()
+            p_copy(d, col).wait_send()
+
         def sent(d, carry):
-            row_copy(d).wait_send()
+            row_copy(d, col).wait_send()
             return carry
         lax.fori_loop(1, n_dev, sent, 0)
-        pltpu.make_async_copy(rowbuf, rows_out.at[col], row_self).wait()
 
     for z in range(width):
         @pl.when((stage < last_stage) | (col != z))
         def _():
             row_copy(1, z).wait_recv()
+
+    first, second = {}, {}
+    for k in range(num_k):
+        for z in range(width):
+            (second if CHUNKS[k][z][1] else first)[CHUNKS[k][z][0]] = (z, k)
+    got = [rland[z].astype(f32) for z in range(width)]
+
+    def row_of(place, odd):
+        return got[place[0]][2 * place[1] + odd:2 * place[1] + odd + 1]
+    batch = dec_out.shape[0]
+    dec_out[...] = jnp.concatenate([row_of(second[p], 1) for p in range(batch)], axis=0).astype(bf16)
+    last_out[...] = jnp.concatenate([jnp.where(lens[p // row_count, p % row_count] > chunk, row_of(second[p], 0), row_of(first[p], 0))
+                                     for p in range(batch)], axis=0).astype(bf16)
 
 
 def solution(mesh):
@@ -414,9 +540,6 @@
     cache_spec = P(None, 'replica', None, TP_AXES, None)
     out_specs = (P('replica', None), P('replica', None), cache_spec, cache_spec)
     num_k = len(CHUNKS)
-    pid_tab = np.array([[c[0] for c in row] for row in CHUNKS], np.int32)
-    half_tab = np.array([[c[1] for c in row] for row in CHUNKS], np.int32)
-
     def shard_body(x_prompt, lengths, x_new, st_qkv, st_out, st_gateup, st_down_t, gain_attn, gain_mlp, tp_query, tp_key, tp_value, tp_out, tp_gate, tp_up, tp_down):
         seq_len, model_dim = x_prompt.shape[2:]
         batch = x_new.shape[0]
@@ -426,44 +549,13 @@
         ff = w_down_t.shape[1]
         chunk = seq_len // 2
         rows = chunk + 16
-        small = 16
-        stage = lax.axis_index('model')
-        col = lax.axis_index('model2')
-        g_attn = lax.dynamic_slice_in_dim(gain_attn, stage, 1, 0)
-        g_mlp = lax.dynamic_slice_in_dim(gain_mlp, stage, 1, 0)
-        lens = lengths.reshape(batch)
-        x_chunks = x_prompt.reshape(batch, 2, chunk, model_dim)
-        pids = jnp.asarray(pid_tab)[:, col]
-        halves = jnp.asarray(half_tab)[:, col]
-        x_mine = jnp.stack([jnp.concatenate([x_chunks[pids[k], halves[k]], x_new[pids[k]][None], jnp.zeros((rows - chunk - 1, model_dim), jnp.bfloat16)], axis=0)
-                            for k in range(num_k)])
-        len_k = lens[pids][:, None]
-        half_k = halves[:, None]
-        row_i = jnp.arange(rows)[None]
-        pos = jnp.where(row_i < chunk, half_k * chunk + row_i, len_k)
-
-        def tables(p):
-            cos_h, sin_h = rope_angles(p, head_dim)
-            return jnp.concatenate([cos_h] * 4, axis=-1), jnp.concatenate([-sin_h, sin_h] * 2, axis=-1)
-
-        def masks(p, dec):
-            j = jnp.arange(KEYS)[None, None]
-            kpos = jnp.where(j < chunk, j, half_k[..., None] * chunk + j - chunk)
-            seen = jnp.where(j < chunk, half_k[..., None] == 1, j < 2 * chunk)
-            m = seen & (kpos < len_k[..., None]) & (dec | (kpos <= p[..., None]))
-            return (m | (dec & (j == 2 * chunk))).astype(jnp.float32)
-
-        cos_t, sin_t = tables(pos)
-        mask = masks(pos, jnp.broadcast_to(row_i >= chunk, pos.shape)[..., None])
-        s_i = jnp.arange(small)[None]
-        is_dec = jnp.broadcast_to(s_i % 2 == 1, (num_k, small))
-        last_i = jnp.clip(len_k - 1 - half_k * chunk, 0, chunk - 1)
-        pick = jnp.where(is_dec, chunk, last_i)
-        mine = s_i // 2 == jnp.arange(num_k)[:, None]
-        sel = (mine[..., None] & (pick[..., None] == row_i[:, None])).astype(jnp.bfloat16)
-        pos_l = jnp.where(is_dec, len_k, half_k * chunk + last_i)
-        cos_l, sin_l = tables(pos_l)
-        mask_l = masks(pos_l, is_dec[..., None])
+        small = 8
+        half_dim = head_dim // 2
+        inv_freq = np.power(np.float32(THETA), np.arange(half_dim, dtype=np.float32) * np.float32(-2.0 / head_dim)).astype(np.float32)
+        angles = (np.arange(seq_len + 8, dtype=np.float32)[:, None] * inv_freq).astype(np.float32)
+        cos_h, sin_h = np.cos(angles).astype(np.float32), np.sin(angles).astype(np.float32)
+        tab_cos = jnp.asarray(np.concatenate([cos_h] * 4, axis=1))
+        tab_sin = jnp.asarray(np.concatenate([-sin_h, sin_h] * 2, axis=1))
 
         dims = (stages, width, num_k, rows, chunk, model_dim, q_cols, ff)
         bf16, f32 = jnp.bfloat16, jnp.float32
@@ -471,12 +563,12 @@
         vm = pl.BlockSpec(memory_space=pltpu.VMEM)
         hbm = pl.BlockSpec(memory_space=pl.ANY)
         dma = pltpu.SemaphoreType.DMA
-        kv_all, rows_all = pl.pallas_call(
+        kv_all, dec, last = pl.pallas_call(
             functools.partial(mega_kernel, dims),
             out_shape=(jax.ShapeDtypeStruct((stages, width, num_k, rows, 128), bf16),
-                       jax.ShapeDtypeStruct((width, small, model_dim), bf16)),
-            in_specs=[hbm] + [vm] * 9 + [hbm] * 4,
-            out_specs=(hbm, hbm),
+                       jax.ShapeDtypeStruct((batch, model_dim), bf16), jax.ShapeDtypeStruct((batch, model_dim), bf16)),
+            in_specs=[pl.BlockSpec(memory_space=pltpu.SMEM), hbm] + [vm] * 5 + [hbm] * 4,
+            out_specs=(hbm, vm, vm),
             scratch_shapes=[
                 pltpu.VMEM((NBUF, model_dim, BLK), bf16),
                 pltpu.VMEM((num_k, rows, model_dim), bf16),
@@ -490,25 +582,32 @@
                 pltpu.VMEM((rows, model_dim), bf16),
                 pltpu.VMEM((rows, model_dim), bf16),
                 pltpu.VMEM((rows, model_dim), f32),
+                pltpu.VMEM((rows, 128), f32),
+                pltpu.VMEM((rows, 128), f32),
+                pltpu.VMEM((rows, KEYS), f32),
+                pltpu.VMEM((small, 128), f32),
+                pltpu.VMEM((small, 128), f32),
+                pltpu.VMEM((small, KEYS), f32),
                 pltpu.VMEM((small, model_dim), bf16),
                 pltpu.VMEM((small, model_dim), f32),
                 pltpu.VMEM((small, q_cols), f32),
+                pltpu.VMEM((width, small, model_dim), bf16),
+                pltpu.VMEM((width, small, model_dim), f32),
+                pltpu.VMEM((width, small, model_dim), f32),
                 pltpu.VMEM((small, model_dim), bf16),
+                pltpu.VMEM((width, small, model_dim), bf16),
                 dma((NBUF,)), dma((num_k,)), dma((num_k,)), dma((num_k * n_dev,)), dma((num_k * n_dev,)), dma((num_k,)),
-                dma, dma, dma((n_dev,)), dma((width,)), dma,
+                dma, dma, dma((n_dev,)), dma((width,)), dma((width,)), dma((width,)), dma((width,)), dma((width,)),
             ],
             compiler_params=pltpu.CompilerParams(collective_id=0, has_side_effects=True, vmem_limit_bytes=67043328),
             name='pipeline',
-        )(x_mine, cos_t, sin_t, mask, sel, cos_l, sin_l, mask_l, g_attn, g_mlp, w_qkv, w_out, w_gateup, w_down_t)
+        )(lengths, x_prompt, x_new, tab_cos, tab_sin, gain_attn, gain_mlp, w_qkv, w_out, w_gateup, w_down_t)
 
         where_a = {}
         where_b = {}
         for k in range(num_k):
             for z in range(width):
                 (where_b if CHUNKS[k][z][1] else where_a)[CHUNKS[k][z][0]] = (z, k)
-        dec = jnp.stack([rows_all[where_b[p][0], 2 * where_b[p][1] + 1] for p in range(batch)])
-        last = jnp.stack([jnp.where(lens[p] > chunk, rows_all[where_b[p][0], 2 * where_b[p][1]], rows_all[where_a[p][0], 2 * where_a[p][1]])
-                          for p in range(batch)])
         full_kv = jnp.stack([jnp.concatenate([kv_all[:, where_a[p][0], where_a[p][1], :chunk],
                                               kv_all[:, where_b[p][0], where_b[p][1], :chunk + 1]], axis=1)
                              for p in range(batch)], axis=1)

time: 334 us -> 269 us (0.81)
  the two profiles are of different devices: /device:TPU:5 before, /device:TPU:0 now
where the time goes in v3:
time: 269 us; the launch traced here: 268 us
  Pallas kernels  254 us (94%)
  local copies, waits for them, and re-layouts  13.8 us (5%)
    pallas_call x1, Pallas kernels, shard_body(): pl.pallas_call(functools.partial(mega_kernel, dims), out_shape=(jax.Shape...  254 us
    unnamed x8, local copies, waits for them, and re-layouts  7.69 us

profile of v3, /device:TPU:0, one launch (start us, length us, event | category | flops | bytes accessed | tf_op | source)
XLA Modules:
  0.0 268.3 jit_solution(15579279909915047391)
XLA Ops:
  0.6 253.6 %pipeline.1 = (bf16[4,4,3,208,128]{4,3,2,1,0:T(8,128)(2,1)}, bf16[6,2048]{1,0:T(8,128)(2,1)}, bf16[6,2048]{1,0:T(8,128)(2,1)}) custom-call(s32[2,3]{1,0:T(2,128)} %lens.1, bf16[2,3,384,2048]{3,2,1,0:T(8,128)(2,1)} %x_prompt.1, bf16[6,2048]{1,0:T(8,128)(2,1)} %x_new.1, f32[392,128]{1,0:T(8,128)} %constant.4.clone.tab_cos, f32[392,128]{1,0:T(8,128)} %constant.5.clone.tab_sin, ...), custom_call_target="tpu_custom_call" | custom-call | tf_op jit(solution)/shard_map/pipeline/pallas_call | solution.py:566
  254.2 1.0 slice_bitcast_fusion.7
  255.2 1.4 slice_bitcast_fusion.2
  256.6 1.4 slice_bitcast_fusion.8
  258.0 0.1 fusion.1
  258.1 0.1 fusion.2
  258.2 0.1 fusion.3
  258.2 0.1 fusion.4
  258.3 0.1 fusion.5
  258.4 2.3 slice_bitcast_fusion
  260.6 4.1 %copy.27 = bf16[4,6,385,1,64]{2,4,3,1,0:T(8,128)(2,1)} copy(bf16[4,6,385,1,64]{4,2,0,1,3:T(8,128)(2,1)} %get-tuple-element.25) | data formatting | bytes 2365440
  264.7 0.0 copy-start.1
  264.7 0.0 copy-start
  264.7 2.4 copy.26
  267.1 0.0 copy-done.1
  267.1 0.6 copy.39
  267.7 0.0 copy-done
  267.7 0.6 copy.40
  (1 shorter events, 0.0 us)
Async XLA Ops:
  264.7 2.4 copy-start.1
  264.7 3.0 %copy-start = (bf16[6,2048]{1,0:T(8,128)(2,1)S(1)}, bf16[6,2048]{1,0:T(8,128)(2,1)}, u32[]{:S(2)}) copy-start(bf16[6,2048]{1,0:T(8,128)(2,1)} %get-tuple-element.32) | copy-start | bytes 73732

commit v4 on v3

--- a/solution.py
+++ b/solution.py
@@ -48,7 +48,7 @@
 
 def mega_kernel(dims, lens, x_prompt, x_new, tab_cos, tab_sin, ga_all, gm_all,
                 w_qkv, w_out, w_gu, w_dt, kv_out, dec_out, last_out,
-                wbuf, xin, ysend, kvst, nb, kst, vst, qbuf, obuf, hbuf, x1buf, yacc, cosb, sinb, maskb, coslb, sinlb, masklb,
+                wbuf, xin, ysend, kvst, nb, kst, vst, qbuf, obuf, hbuf, x1buf, yacc, abuf, cosb, sinb, maskb, coslb, sinlb, masklb,
                 hsel, x6, o6, hg, yparts, yrecv, rowbuf, rland,
                 wsem, act_send, act_recv, kv_send, kv_recv, kv_self, nb_send, nb_recv, row_send, row_recv,
                 h_send, h_recv, p_send, p_recv):
@@ -83,9 +83,11 @@
         return lax.broadcasted_iota(jnp.int32, shape, dim)
 
     def visible(j, pos, dec, length, half):
-        kpos = jnp.where(j < chunk, j, half * chunk + j - chunk)
-        seen = (j >= chunk * (1 - half)) & (j < 2 * chunk) & (kpos < length) & (dec | (kpos <= pos))
-        return jnp.where(seen | (dec & (j == 2 * chunk)), 1.0, 0.0)
+        ctx = KEYS // 2
+        kpos = jnp.where(j < ctx, half * chunk + j, j - ctx)
+        there = (j < chunk) | ((j >= ctx) & (j < ctx + half * chunk))
+        seen = there & (kpos < length) & (dec | (kpos <= pos))
+        return jnp.where(seen | (dec & (j == chunk)), 1.0, 0.0)
 
     def set_tables(k):
         length, half = here(k, len_tab), here(k, half_tab)
@@ -296,7 +298,7 @@
                 packed = jnp.where(low, pltpu.roll(kt, 64, 1), vt)
             packed = packed.astype(bf16)
             kvst[k, c] = packed
-            stack(c, chunk, packed.astype(f32))
+            stack(c, 0, packed.astype(f32))
 
         @pl.when(k == 0)
         def _():
@@ -314,30 +316,42 @@
         def _():
             nb_copy().wait_recv()
             for c in range(stages):
-                stack(c, 0, nb[c, :chunk].astype(f32))
+                stack(c, KEYS // 2, nb[c, :chunk].astype(f32))
 
         @pl.when((k > 0) & jnp.logical_not(use_nb))
         def _():
             for c in range(stages):
-                stack(c, 0, kvst[lax.max(k - 1, 0), c, :chunk].astype(f32))
-
-    def attend(q_ref, o_ref, m_ref, n_rows):
-        pairs = q_cols // 128
-        per_c = pairs // stages
-
-        def pair(i, carry):
-            c = i // per_c
-            at = pl.ds(pl.multiple_of(i * 128, 128), 128)
-            s = dot32t(q_ref[:, at], kst[c])
-            parts = []
-            for e in range(2):
-                se = jnp.where(m_ref[...] > 0.5, s[:, e * KEYS:(e + 1) * KEYS], NEG)
-                ex = jnp.exp(se - jnp.max(se, axis=-1, keepdims=True))
-                inv = 1.0 / jnp.sum(ex, axis=-1, keepdims=True)
-                parts.append((ex * inv).astype(bf16))
-            o_ref[:, at] = dot32(jnp.concatenate(parts, axis=1), vst[c]).astype(bf16)
+                stack(c, KEYS // 2, kvst[lax.max(k - 1, 0), c, :chunk].astype(f32))
+
+    def attend(q_ref, o_ref, m_ref, n_keys):
+        per_c = q_cols // 128 // stages
+
+        def group(c, carry):
+            for i in range(per_c):
+                at = pl.ds(pl.multiple_of((c * per_c + i) * 128, 128), 128)
+                q = q_ref[:, at]
+                out = None
+                for e in range(2):
+                    ks = slice(e * KEYS, e * KEYS + n_keys)
+                    se = jnp.where(m_ref[:, :n_keys] > 0.5, dot32t(q, kst[c, ks]), NEG)
+                    ex = jnp.exp(se - jnp.max(se, axis=-1, keepdims=True))
+                    inv = 1.0 / jnp.sum(ex, axis=-1, keepdims=True)
+                    part = dot32((ex * inv).astype(bf16), vst[c, ks])
+                    out = part if out is None else out + part
+                o_ref[:, at] = out.astype(bf16)
             return carry
-        lax.fori_loop(0, pairs, pair, 0)
+        lax.fori_loop(0, stages, group, 0)
+
+    def attend_chunk(k, q_ref, o_ref, m_ref):
+        half = here(k, half_tab)
+
+        @pl.when(half == 0)
+        def _():
+            attend(q_ref, o_ref, m_ref, KEYS // 2)
+
+        @pl.when(half == 1)
+        def _():
+            attend(q_ref, o_ref, m_ref, KEYS)
 
     scale = 64 ** -0.5
 
@@ -371,7 +385,7 @@
                 return cc
             lax.fori_loop(0, n_q, q_block, 0)
 
-            attend(qbuf, obuf, maskb, rows)
+            attend_chunk(k, qbuf, obuf, maskb)
 
             def o_block(j, cc):
                 g = g0 + 1 + n_q + j
@@ -386,19 +400,38 @@
             hbuf[...] = norm_rows(x1, gm_ref[...])
             yacc[...] = jnp.zeros_like(yacc)
 
-            def f_block(j, cc):
-                g = g0 + 1 + n_q + n_o + 3 * j
-                sg = landed(g)
-                su = landed(g + 1)
-                kv_copy(k, 1 + n_o + j, me).start()
-                a = act_of(hbuf[...], sg, su)
-                refill(g, total)
-                refill(g + 1, total)
-                sd = landed(g + 2)
-                yacc[...] += dot32t(a, wbuf[sd])
-                refill(g + 2, total)
+            gf = g0 + 1 + n_q + n_o
+
+            def up(j, slot):
+                abuf[slot] = act_of(hbuf[...], wslot(gf + 3 * j), wslot(gf + 3 * j + 1))
+
+            def down(j, slot):
+                yacc[...] += dot32t(abuf[slot], wbuf[wslot(gf + 3 * j + 2)])
+
+            landed(gf)
+            landed(gf + 1)
+            up(0, 0)
+            refill(gf, total)
+            refill(gf + 1, total)
+
+            def f_pair(t, cc):
+                j = 2 * t + 1
+                for b in range(6):
+                    landed(gf + 3 * j - 1 + b)
+                kv_copy(k, n_o + j, me).start()
+                kv_copy(k, n_o + j + 1, me).start()
+                up(j, 1)
+                down(j - 1, 0)
+                up(j + 1, 0)
+                down(j, 1)
+                for b in range(6):
+                    refill(gf + 3 * j - 1 + b, total)
                 return cc
-            lax.fori_loop(0, n_f, f_block, 0)
+            lax.fori_loop(0, n_f // 2, f_pair, 0)
+            kv_copy(k, n_dev - 1, me).start()
+            landed(gf + 3 * n_f - 1)
+            down(n_f - 1, 0)
+            refill(gf + 3 * n_f - 1, total)
             ysend[k] = (x1buf[...].astype(f32) + yacc[...]).astype(bf16)
             act_copy(k).start()
             return carry
@@ -435,7 +468,7 @@
                     qbuf[:small, pl.ds(pl.multiple_of(j * BLK + i * 128, 128), 128)] = (v[i] * scale).astype(bf16)
                 return cc
             lax.fori_loop(0, n_q, q_block, 0)
-            attend(qbuf.at[:small], obuf.at[:small], masklb, small)
+            attend(qbuf.at[:small], obuf.at[:small], masklb, KEYS)
             o6[...] = jnp.where(row_id // 2 == k, obuf[:small].astype(f32), o6[...])
             return carry
         lax.fori_loop(0, num_k, one_chunk, 0)
@@ -582,6 +615,7 @@
                 pltpu.VMEM((rows, model_dim), bf16),
                 pltpu.VMEM((rows, model_dim), bf16),
                 pltpu.VMEM((rows, model_dim), f32),
+                pltpu.VMEM((2, rows, BLK), bf16),
                 pltpu.VMEM((rows, 128), f32),
                 pltpu.VMEM((rows, 128), f32),
                 pltpu.VMEM((rows, KEYS), f32),

time: 269 us -> 248 us (0.922)
  Pallas kernels: 254 us -> 233 us
    pallas_call x1, Pallas kernels: 254 us -> 233 us  [shard_body(): pl.pallas_call(functools.partial(mega_kernel, dims), out_shape=(jax.Shape...]
where the time goes in v4:
time: 248 us; the launch traced here: 247 us
  Pallas kernels  233 us (94%)
  local copies, waits for them, and re-layouts  13.8 us (6%)
    pallas_call x1, Pallas kernels, shard_body(): pl.pallas_call(functools.partial(mega_kernel, dims), out_shape=(jax.Shape...  233 us
    unnamed x8, local copies, waits for them, and re-layouts  7.69 us

profile of v4, /device:TPU:0, one launch (start us, length us, event | category | flops | bytes accessed | tf_op | source)
XLA Modules:
  0.0 247.3 jit_solution(3746904448531136345)
XLA Ops:
  0.6 232.6 %pipeline.1 = (bf16[4,4,3,208,128]{4,3,2,1,0:T(8,128)(2,1)}, bf16[6,2048]{1,0:T(8,128)(2,1)}, bf16[6,2048]{1,0:T(8,128)(2,1)}) custom-call(s32[2,3]{1,0:T(2,128)} %lens.1, bf16[2,3,384,2048]{3,2,1,0:T(8,128)(2,1)} %x_prompt.1, bf16[6,2048]{1,0:T(8,128)(2,1)} %x_new.1, f32[392,128]{1,0:T(8,128)} %constant.4.clone.tab_cos, f32[392,128]{1,0:T(8,128)} %constant.5.clone.tab_sin, ...), custom_call_target="tpu_custom_call" | custom-call | tf_op jit(solution)/shard_map/pipeline/pallas_call | solution.py:599
  233.2 1.0 slice_bitcast_fusion.7
  234.2 1.4 slice_bitcast_fusion.2
  235.6 1.4 slice_bitcast_fusion.8
  237.1 0.1 fusion.1
  237.1 0.1 fusion.2
  237.2 0.1 fusion.3
  237.2 0.1 fusion.4
  237.3 0.1 fusion.5
  237.4 2.3 slice_bitcast_fusion
  239.6 4.1 %copy.27 = bf16[4,6,385,1,64]{2,4,3,1,0:T(8,128)(2,1)} copy(bf16[4,6,385,1,64]{4,2,0,1,3:T(8,128)(2,1)} %get-tuple-element.25) | data formatting | bytes 2365440
  243.7 0.0 copy-start.1
  243.7 0.0 copy-start
  243.8 2.4 copy.26
  246.1 0.0 copy-done.1
  246.1 0.6 copy.39
  246.7 0.0 copy-done
  246.7 0.6 copy.40
  (1 shorter events, 0.0 us)
Async XLA Ops:
  243.7 2.4 copy-start.1
  243.7 3.0 %copy-start = (bf16[6,2048]{1,0:T(8,128)(2,1)S(1)}, bf16[6,2048]{1,0:T(8,128)(2,1)}, u32[]{:S(2)}) copy-start(bf16[6,2048]{1,0:T(8,128)(2,1)} %get-tuple-element.32) | copy-start | bytes 73732

commit v5 on v4

--- a/solution.py
+++ b/solution.py
@@ -280,8 +280,12 @@
         lo = low[:n]
         turned = pltpu.roll(packed, 64, 1)
         zero = jnp.zeros_like(packed)
-        kst[c, base:base + n, :] = jnp.where(lo, packed, zero).astype(bf16)
-        kst[c, KEYS + base:KEYS + base + n, :] = jnp.where(lo, zero, turned).astype(bf16)
+        both = jnp.concatenate([packed, jnp.zeros((256 - n, 128), f32)], axis=0).T[:64]
+        none = jnp.zeros_like(both)
+        kst[c, :64, base:base + 256] = both.astype(bf16)
+        kst[c, 64:, base:base + 256] = none.astype(bf16)
+        kst[c, :64, KEYS + base:KEYS + base + 256] = none.astype(bf16)
+        kst[c, 64:, KEYS + base:KEYS + base + 256] = both.astype(bf16)
         vst[c, base:base + n, :] = jnp.where(lo, turned, zero).astype(bf16)
         vst[c, KEYS + base:KEYS + base + n, :] = jnp.where(lo, zero, packed).astype(bf16)
 
@@ -323,35 +327,36 @@
             for c in range(stages):
                 stack(c, KEYS // 2, kvst[lax.max(k - 1, 0), c, :chunk].astype(f32))
 
-    def attend(q_ref, o_ref, m_ref, n_keys):
-        per_c = q_cols // 128 // stages
-
+    per_c = q_cols // 128 // stages
+
+    def attend(o_ref, m_ref, n_rows, n_keys):
         def group(c, carry):
-            for i in range(per_c):
-                at = pl.ds(pl.multiple_of((c * per_c + i) * 128, 128), 128)
-                q = q_ref[:, at]
-                out = None
-                for e in range(2):
-                    ks = slice(e * KEYS, e * KEYS + n_keys)
-                    se = jnp.where(m_ref[:, :n_keys] > 0.5, dot32t(q, kst[c, ks]), NEG)
+            q = qbuf[c, :per_c * n_rows]
+            seen = m_ref[:, :n_keys] > 0.5
+            probs = []
+            for e in range(2):
+                s_all = dot32(q, kst[c, :, e * KEYS:e * KEYS + n_keys])
+                for i in range(per_c):
+                    se = jnp.where(seen, s_all[i * n_rows:(i + 1) * n_rows], NEG)
                     ex = jnp.exp(se - jnp.max(se, axis=-1, keepdims=True))
                     inv = 1.0 / jnp.sum(ex, axis=-1, keepdims=True)
-                    part = dot32((ex * inv).astype(bf16), vst[c, ks])
-                    out = part if out is None else out + part
-                o_ref[:, at] = out.astype(bf16)
+                    probs.append((ex * inv).astype(bf16))
+            out = dot32(jnp.concatenate(probs[:per_c], axis=0), vst[c, :n_keys]) + dot32(jnp.concatenate(probs[per_c:], axis=0), vst[c, KEYS:KEYS + n_keys])
+            for i in range(per_c):
+                o_ref[:, pl.ds(pl.multiple_of((c * per_c + i) * 128, 128), 128)] = out[i * n_rows:(i + 1) * n_rows].astype(bf16)
             return carry
         lax.fori_loop(0, stages, group, 0)
 
-    def attend_chunk(k, q_ref, o_ref, m_ref):
+    def attend_chunk(k, o_ref, m_ref):
         half = here(k, half_tab)
 
         @pl.when(half == 0)
         def _():
-            attend(q_ref, o_ref, m_ref, KEYS // 2)
+            attend(o_ref, m_ref, rows, KEYS // 2)
 
         @pl.when(half == 1)
         def _():
-            attend(q_ref, o_ref, m_ref, KEYS)
+            attend(o_ref, m_ref, rows, KEYS)
 
     scale = 64 ** -0.5
 
@@ -380,12 +385,12 @@
                 slot = landed(g)
                 v = rope_block(dot32(hbuf[...], wbuf[slot]), cosb[...], sinb[...])
                 for i in range(BLK // 128):
-                    qbuf[:, pl.ds(pl.multiple_of(j * BLK + i * 128, 128), 128)] = (v[i] * scale).astype(bf16)
+                    qbuf[j, i * rows:(i + 1) * rows] = (v[i] * scale).astype(bf16)
                 refill(g, total)
                 return cc
             lax.fori_loop(0, n_q, q_block, 0)
 
-            attend_chunk(k, qbuf, obuf, maskb)
+            attend_chunk(k, obuf, maskb)
 
             def o_block(j, cc):
                 g = g0 + 1 + n_q + j
@@ -464,11 +469,10 @@
 
             def q_block(j, cc):
                 v = rope_block(dot32(hs, wbuf[1 + j]), coslb[...], sinlb[...])
-                for i in range(BLK // 128):
-                    qbuf[:small, pl.ds(pl.multiple_of(j * BLK + i * 128, 128), 128)] = (v[i] * scale).astype(bf16)
+                qbuf[j, :per_c * small] = (jnp.concatenate(v, axis=0) * scale).astype(bf16)
                 return cc
             lax.fori_loop(0, n_q, q_block, 0)
-            attend(qbuf.at[:small], obuf.at[:small], masklb, KEYS)
+            attend(obuf.at[:small], masklb, small, KEYS)
             o6[...] = jnp.where(row_id // 2 == k, obuf[:small].astype(f32), o6[...])
             return carry
         lax.fori_loop(0, num_k, one_chunk, 0)
@@ -608,9 +612,9 @@
                 pltpu.VMEM((num_k, rows, model_dim), bf16),
                 pltpu.VMEM((num_k, stages, rows, 128), bf16),
                 pltpu.VMEM((stages, rows, 128), bf16),
+                pltpu.VMEM((stages, 128, 2 * KEYS), bf16),
                 pltpu.VMEM((stages, 2 * KEYS, 128), bf16),
-                pltpu.VMEM((stages, 2 * KEYS, 128), bf16),
-                pltpu.VMEM((rows, q_cols), bf16),
+                pltpu.VMEM((stages, q_cols // 128 // stages * rows, 128), bf16),
                 pltpu.VMEM((rows, q_cols), bf16),
                 pltpu.VMEM((rows, model_dim), bf16),
                 pltpu.VMEM((rows, model_dim), bf16),

time: 248 us -> 234 us (0.944)
  Pallas kernels: 233 us -> 219 us
    pallas_call x1, Pallas kernels: 233 us -> 219 us  [shard_body(): pl.pallas_call(functools.partial(mega_kernel, dims), out_shape=(jax.Shape...]
where the time goes in v5:
time: 234 us; the launch traced here: 233 us
  Pallas kernels  219 us (94%)
  local copies, waits for them, and re-layouts  13.8 us (6%)
    pallas_call x1, Pallas kernels, shard_body(): pl.pallas_call(functools.partial(mega_kernel, dims), out_shape=(jax.Shape...  219 us
    unnamed x8, local copies, waits for them, and re-layouts  7.69 us

profile of v5, /device:TPU:0, one launch (start us, length us, event | category | flops | bytes accessed | tf_op | source)
XLA Modules:
  0.0 233.4 jit_solution(6561082169275157053)
XLA Ops:
  0.6 218.6 %pipeline.1 = (bf16[4,4,3,208,128]{4,3,2,1,0:T(8,128)(2,1)}, bf16[6,2048]{1,0:T(8,128)(2,1)}, bf16[6,2048]{1,0:T(8,128)(2,1)}) custom-call(s32[2,3]{1,0:T(2,128)} %lens.1, bf16[2,3,384,2048]{3,2,1,0:T(8,128)(2,1)} %x_prompt.1, bf16[6,2048]{1,0:T(8,128)(2,1)} %x_new.1, f32[392,128]{1,0:T(8,128)} %constant.4.clone.tab_cos, f32[392,128]{1,0:T(8,128)} %constant.5.clone.tab_sin, ...), custom_call_target="tpu_custom_call" | custom-call | tf_op jit(solution)/shard_map/pipeline/pallas_call | solution.py:603
  219.2 1.0 slice_bitcast_fusion.7
  220.2 1.4 slice_bitcast_fusion.2
  221.6 1.4 slice_bitcast_fusion.8
  223.1 0.1 fusion.1
  223.2 0.1 fusion.2
  223.2 0.1 fusion.3
  223.3 0.1 fusion.4
  223.3 0.1 fusion.5
  223.4 2.3 slice_bitcast_fusion
  225.7 4.1 %copy.27 = bf16[4,6,385,1,64]{2,4,3,1,0:T(8,128)(2,1)} copy(bf16[4,6,385,1,64]{4,2,0,1,3:T(8,128)(2,1)} %get-tuple-element.25) | data formatting | bytes 2365440
  229.8 0.0 copy-start.1
  229.8 0.0 copy-start
  229.8 2.4 %copy.26 = bf16[4,6,385,1,64]{2,4,3,1,0:T(8,128)(2,1)} copy(bf16[4,6,385,1,64]{4,2,0,1,3:T(8,128)(2,1)S(1)} %get-tuple-element.26) | data formatting | bytes 2365440
  232.1 0.0 copy-done.1
  232.1 0.6 copy.39
  232.8 0.0 copy-done
  232.8 0.6 copy.40
  (1 shorter events, 0.0 us)
Async XLA Ops:
  229.8 2.4 %copy-start.1 = (bf16[6,2048]{1,0:T(8,128)(2,1)S(1)}, bf16[6,2048]{1,0:T(8,128)(2,1)}, u32[]{:S(2)}) copy-start(bf16[6,2048]{1,0:T(8,128)(2,1)} %get-tuple-element.31) | copy-start | bytes 73732
  229.8 3.0 %copy-start = (bf16[6,2048]{1,0:T(8,128)(2,1)S(1)}, bf16[6,2048]{1,0:T(8,128)(2,1)}, u32[]{:S(2)}) copy-start(bf16[6,2048]{1,0:T(8,128)(2,1)} %get-tuple-element.32) | copy-start | bytes 73732
